TPU v7x, 32 devices: a whole 2x2x4 slice. The times are simulated.
32 devices in a mesh: rep: 2 (over x), shard: 16 (over z, y, core).
Axes of the slice: x: 2, y: 2, z: 4, core: 2. Of those that a mesh axis runs over, the one named last changes fastest.
Arguments:
- dense: bfloat16 [8192, 128], P(('rep', 'shard')), may hold values from -6 to 6
- small_ids: int32 [8192, 32], P(('rep', 'shard')), may hold values from 0 to 511
- labels: int32 [8192], P(('rep', 'shard')), may hold values 0 or 1
- small_tables: bfloat16 [32, 512, 128], replicated, may hold values from -6 to 6
- large_tables: bfloat16 [16, 8192, 128], P('shard'), may hold values from -6 to 6
- batch_sizes: int32 [16, 32], replicated, may hold values from 1 to 128, as said below
- bag_ends: int32 [16, 32, 128], P('shard'), may hold values from 0 to 256, as said below
- owner_row_index: int32 [16, 32, 256], P('shard'), may hold values from 0 to 8191
- w_first: bfloat16 [1304, 1024], replicated, may hold values from -0.15625 to 0.15625
- b_first: float32 [1024], replicated, may hold values from -3 to 3
- w_out: float32 [1024], replicated, may hold values from -0.1875 to 0.1875
Outputs:
- small_new: bfloat16 [32, 512, 128], replicated
- large_new: bfloat16 [16, 8192, 128], P('shard')
Inputs may be any that keep to these rules, and one draw needn't show every extreme that they name: `batch_sizes`: every feature has some owner, and every owner some feature, with exactly 128. `bag_ends`: nondecreasing along the last dimension; bags j >= batch_sizes[f, d] are empty; some bag list reaches 256.
All inputs are finite; a program needn't handle non-finite values. No bound on the sum of `labels` on one device may be relied on, other than what follows from the above.
Results may differ from a plain program's by a relative error of at most 0.0095.
Values may be sent and summed in bfloat16 or wider, within the bound.
A program may use at most 192 MiB of HBM per device.

v0:
```python
import jax
import jax.numpy as jnp
from jax import lax
from jax.sharding import PartitionSpec as P

step_size = 32.0


def as_sent(array):

    def short(part):
        return part.astype(jnp.bfloat16) if part.dtype == jnp.float32 else part

    return jax.tree.map(short, array)


def bag_members(limits, slot_total):
    starts = jnp.concatenate(
        [jnp.zeros(limits.shape[:-1] + (1,), jnp.int32), limits[..., :-1]], axis=-1
    )
    positions = jnp.arange(slot_total, dtype=jnp.int32)
    inside = (positions >= starts[..., None]) & (positions < limits[..., None])
    return inside.astype(jnp.bfloat16)


def silu_slope(preacts):
    squash = jax.nn.sigmoid(preacts)
    return squash * (1.0 + preacts * (1.0 - squash))


def spread_table(size_table, batch_rows, bag_span):
    chosen = jnp.arange(batch_rows, dtype=jnp.int32) * size_table[..., None] // batch_rows
    return (chosen[..., None] == jnp.arange(bag_span, dtype=jnp.int32)).astype(jnp.bfloat16)


def take_rows(table_one, row_list):
    return table_one[row_list]


def lower_pairs(gram_matrix, vec_count):
    pieces = [gram_matrix[:, index, :index] for index in range(1, vec_count)]
    return jnp.concatenate(pieces, axis=1)


def lower_square(pair_grad, vec_count):
    rows_list = []
    offset = 0
    for index in range(vec_count):
        piece = pair_grad[:, offset : offset + index]
        offset = offset + index
        rows_list.append(jnp.pad(piece, ((0, 0), (0, vec_count - index))))
    return jnp.stack(rows_list, axis=1)


def table_grads(row_list, members, gradient_list, row_total):
    slot_vectors = jnp.einsum(
        "fdks,fdke->fdse", members, gradient_list, preferred_element_type=jnp.float32
    )
    embed_width = gradient_list.shape[-1]

    def one_table(values, row_index):
        return jax.ops.segment_sum(
            values.reshape(-1, embed_width), row_index.reshape(-1), row_total
        )

    return jax.vmap(one_table)(slot_vectors, row_list)


def shards(
    dense,
    small_ids,
    labels,
    small_tables,
    large_tables,
    batch_sizes,
    bag_ends,
    owner_row_index,
    w_first,
    b_first,
    w_out,
):
    groups = lax.axis_size("shard")
    replica = lax.axis_index("rep")
    member_id = lax.axis_index("shard")
    batch_rows, embed_width = dense.shape
    owned_tables, embedding_rows = (large_tables.shape[0], large_tables.shape[1])
    small_count, small_rows = (small_tables.shape[0], small_tables.shape[1])
    feat_count = batch_sizes.shape[0]
    bag_span = bag_ends.shape[2]
    slot_total = owner_row_index.shape[2]
    pair_count = w_first.shape[0] - embed_width
    vec_count = 1 + small_count + feat_count
    first_dest = replica * groups
    own_limits = lax.dynamic_slice_in_dim(bag_ends, first_dest, groups, 1)
    own_rows = lax.dynamic_slice_in_dim(owner_row_index, first_dest, groups, 1)
    send_sizes = lax.dynamic_slice(
        batch_sizes, (member_id * owned_tables, first_dest), (owned_tables, groups)
    )
    members = bag_members(own_limits, slot_total)
    collected_rows = jax.vmap(take_rows)(large_tables, own_rows)
    pooled = jnp.einsum(
        "fdks,fdse->fdke", members, collected_rows, preferred_element_type=jnp.float32
    ).astype(jnp.bfloat16)
    send_spread = spread_table(send_sizes, batch_rows, bag_span)
    expanded = jnp.einsum(
        "fdbj,fdje->fdbe", send_spread, pooled, preferred_element_type=jnp.float32
    ).astype(jnp.bfloat16)
    arrived = lax.all_to_all(expanded, "shard", split_axis=1, concat_axis=0, tiled=True)
    large_feat = jnp.transpose(arrived[:, 0], (1, 0, 2))
    small_hot = (small_ids[:, :, None] == jnp.arange(small_rows, dtype=jnp.int32)).astype(
        jnp.bfloat16
    )
    minor_feature = jnp.einsum(
        "btr,tre->bte", small_hot, small_tables, preferred_element_type=jnp.float32
    ).astype(jnp.bfloat16)
    vectors = jnp.concatenate([dense[:, None, :], minor_feature, large_feat], axis=1)
    gram_matrix = jnp.einsum("bie,bje->bij", vectors, vectors, preferred_element_type=jnp.float32)
    pair_values = (lower_pairs(gram_matrix, vec_count) * embed_width ** (-0.5)).astype(jnp.bfloat16)
    features = jnp.concatenate([pair_values, dense], axis=1)
    preact = jnp.dot(features, w_first, preferred_element_type=jnp.float32) + b_first
    hidden = jax.nn.silu(preact)
    logits = jnp.sum(hidden * w_out[None, :], axis=1)
    logit_grad = jax.nn.sigmoid(logits) - labels.astype(jnp.float32)
    pre_grad = (logit_grad[:, None] * w_out[None, :] * silu_slope(preact)).astype(jnp.bfloat16)
    pair_grad = jnp.einsum(
        "bh,ph->bp", pre_grad, w_first[:pair_count], preferred_element_type=jnp.float32
    ) * embed_width ** (-0.5)
    lower_part = lower_square(pair_grad, vec_count)
    symmetric = lower_part + jnp.swapaxes(lower_part, 1, 2)
    vec_grad = jnp.einsum("bij,bje->bie", symmetric, vectors.astype(jnp.float32)).astype(
        jnp.bfloat16
    )
    small_local = jnp.einsum(
        "btr,bte->tre",
        small_hot,
        vec_grad[:, 1 : 1 + small_count],
        preferred_element_type=jnp.float32,
    )
    shard_sum = lax.psum_scatter(
        small_local.reshape(small_count * small_rows, embed_width),
        ("rep", "shard"),
        scatter_dimension=0,
        tiled=True,
    )
    part_rows = shard_sum.shape[0]
    flat_tables = small_tables.reshape(small_count * small_rows, embed_width)
    local_rows = lax.dynamic_slice_in_dim(
        flat_tables, lax.axis_index(("rep", "shard")) * part_rows, part_rows, 0
    )
    updated = (local_rows.astype(jnp.float32) - step_size * shard_sum).astype(jnp.bfloat16)
    small_new = lax.all_gather(updated, ("rep", "shard"), axis=0, tiled=True).reshape(
        small_count, small_rows, embed_width
    )
    large_grad_part = vec_grad[:, 1 + small_count :]
    returned = lax.all_to_all(
        jnp.transpose(large_grad_part, (1, 0, 2))[:, None],
        "shard",
        split_axis=0,
        concat_axis=1,
        tiled=True,
    )
    accumulate_gradient = jnp.einsum(
        "fdbj,fdbe->fdje", send_spread, returned, preferred_element_type=jnp.float32
    ).astype(jnp.bfloat16)
    local_grad = table_grads(own_rows, members, accumulate_gradient, embedding_rows)
    large_grad = jax.tree.map(
        lambda part: part.astype(jnp.float32), lax.psum(as_sent(local_grad), "rep")
    )
    large_new = (large_tables.astype(jnp.float32) - step_size * large_grad).astype(jnp.bfloat16)
    return (small_new, large_new)


def solution(mesh):
    placed = (
        P(("rep", "shard"), None),
        P(("rep", "shard"), None),
        P(("rep", "shard")),
        P(),
        P("shard", None, None),
        P(),
        P("shard", None, None),
        P("shard", None, None),
        P(),
        P(),
        P(),
    )
    return jax.shard_map(
        shards, mesh=mesh, in_specs=placed, out_specs=(P(), P("shard", None, None)), check_vma=False
    )
```

profile of v0, /device:TPU:0, one launch (start us, length us, event | category | flops | bytes accessed | tf_op | source)
XLA Modules:
  0.0 441.6 jit_solution(3575104264538039159)
XLA Ops:
  8.7 0.8 pad_bitcast_fusion.1
  10.4 48.0 %gather_fusion = bf16[4096,128]{1,0:T(8,128)(2,1)S(1)} fusion(bf16[1,8192,128]{2,1,0:T(8,128)(2,1)} %param.15, s32[4096]{0:T(1024)S(1)} %bitcast.282), kind=kCustom, calls=%fused_computation | custom fusion | bytes 2129920 | tf_op jit(solution)/shard_map/vmap()/gather | solution.py:37
  58.4 2.3 fusion.26
  60.7 7.6 %all-to-all-start = ((bf16[1,16,256,128]{3,2,0,1:T(8,128)(2,1)}), bf16[1,16,256,128]{3,2,0,1:T(8,128)(2,1)S(1)}, u32[]{:S(2)}, u32[]{:S(2)}) async-start(bf16[1,16,256,128]{3,2,0,1:T(8,128)(2,1)} %fusion.26), calls=%async_computation | async-start | bytes 2097152 | tf_op jit(solution)/shard_map/all_to_all | solution.py:108
  69.4 8.1 %convert_bitcast_fusion.1 = bf16[256,32,128]{2,0,1:T(8,128)(2,1)} fusion(bf16[32,512,128]{2,1,0:T(8,128)(2,1)} %param.14, s32[256,32]{0,1:T(8,128)S(1)} %copy-done.17), kind=kOutput, calls=%fused_computation.27 | convolution fusion | flops 1078984704 | bytes 6324224 | tf_op jit(solution)/shard_map/btr,tre->bte/dot_general | solution.py:113
  77.5 13.8 %all-to-all-done = bf16[1,16,256,128]{3,2,0,1:T(8,128)(2,1)S(1)} async-done(((bf16[1,16,256,128]{3,2,0,1:T(8,128)(2,1)}), bf16[1,16,256,128]{3,2,0,1:T(8,128)(2,1)S(1)}, u32[]{:S(2)}, u32[]{:S(2)}) %all-to-all-start) | async-done | bytes 1048608 | tf_op jit(solution)/shard_map/all_to_all | solution.py:108
  91.2 1.0 copy-done.4
  92.2 2.3 pad_maximum_fusion
  94.5 2.6 fusion.7
  97.3 0.8 slice.407
  98.1 0.8 slice.408
  98.9 0.8 slice.409
  105.0 0.8 slice.417
  105.7 0.8 slice.418
  106.5 0.8 slice.419
  108.0 0.8 slice.421
  108.8 0.8 slice.422
  114.1 0.8 slice.429
  117.2 0.8 slice.433
  120.2 0.8 slice.437
  121.0 0.8 slice.438
  122.5 0.8 slice.440
  123.3 1.3 slice.441
  128.3 0.8 slice.447
  130.6 0.8 slice.450
  131.4 0.8 slice.451
  132.9 5.1 %concatenate.14 = f32[256,1176]{1,0:T(8,128)} concatenate(f32[256,1]{1,0:T(8,128)S(1)} %bitcast.287, f32[256,2]{1,0:T(8,128)S(1)} %bitcast.288, f32[256,3]{1,0:T(8,128)} %bitcast.289, f32[256,4]{1,0:T(8,128)} %bitcast.290, f32[256,5]{1,0:T(8,128)} %bitcast.291, f32[256,6]{1,0:T(8,128)} %bitcast.292, f32[256,7]{1,0:T(8,128)} %bitcast.293, f32[256,8]{1,0:T(8,128)} %bitcast.294, ...), dimensions={1} | concatenate | bytes 2408448 | tf_op jit(solution)/shard_map/concatenate | solution.py:42
  138.1 1.6 multiply_convert_fusion
  139.7 3.0 multiply_reduce_fusion
  142.7 1.2 convolution_multiply_fusion
  180.8 8.3 %copy.224 = f32[256,49,49]{1,0,2:T(8,128)} copy(f32[256,49,49]{2,0,1:T(8,128)} %bitcast_dynamic-update-slice_fusion) | data formatting | bytes 4917248 | tf_op jit(solution)/shard_map/stack | solution.py:52
  189.1 5.9 %bitcast_add_fusion = bf16[256,49,49]{2,0,1:T(8,128)(2,1)S(1)} fusion(f32[256,49,49]{2,0,1:T(8,128)} %bitcast_dynamic-update-slice_fusion, f32[256,49,49]{1,0,2:T(8,128)} %copy.224), kind=kLoop, calls=%fused_computation.9 | loop fusion | flops 1229312 | bytes 6146560 | tf_op jit(solution)/shard_map/add | solution.py:129
  195.1 4.5 %fusion.9 = bf16[256,49,128]{2,1,0:T(8,128)(2,1)S(1)} fusion(bf16[256,49,128]{2,0,1:T(8,128)(2,1)S(1)} %pad_maximum_fusion, bf16[256,49,49]{2,0,1:T(8,128)(2,1)S(1)} %bitcast_add_fusion), kind=kOutput, calls=%fused_computation.16 | convolution fusion | flops 157351936 | bytes 7651840 | tf_op jit(solution)/shard_map/bij,bje->bie/dot_general | solution.py:130
  199.6 1.8 copy-done.3
  201.4 1.2 slice.501
  202.6 6.3 %fusion = f32[32,512,128]{2,1,0:T(8,128)} fusion(s32[256,32]{0,1:T(8,128)S(1)} %copy-done.18, bf16[256,32,128]{2,1,0:T(8,128)(2,1)S(1)} %slice.501), kind=kOutput, calls=%fused_computation.3 | convolution fusion | flops 1077936128 | bytes 10518528 | tf_op jit(solution)/shard_map/btr,bte->tre/dot_general | solution.py:133
  208.9 2.0 slice_bitcast_fusion
  210.9 1.2 copy.228
  212.1 6.8 %all-to-all-start.1 = ((bf16[16,1,256,128]{3,2,1,0:T(8,128)(2,1)}), bf16[16,1,256,128]{3,2,1,0:T(8,128)(2,1)S(1)}, u32[]{:S(2)}, u32[]{:S(2)}) async-start(bf16[16,1,256,128]{3,2,1,0:T(8,128)(2,1)} %copy.228), calls=%async_computation.2 | async-start | bytes 2097152 | tf_op jit(solution)/shard_map/all_to_all | solution.py:155
  219.5 29.3 %all-to-all-done.1 = bf16[16,1,256,128]{3,2,1,0:T(8,128)(2,1)S(1)} async-done(((bf16[16,1,256,128]{3,2,1,0:T(8,128)(2,1)}), bf16[16,1,256,128]{3,2,1,0:T(8,128)(2,1)S(1)}, u32[]{:S(2)}, u32[]{:S(2)}) %all-to-all-start.1) | async-done | bytes 1048608 | tf_op jit(solution)/shard_map/all_to_all | solution.py:155
  248.8 2.4 fusion.21
  251.2 25.0 %scatter_custom_fusion = f32[8192,128]{1,0:T(8,128)} fusion(s32[4096]{0:T(1024)S(1)} %broadcast_select_fusion, f32[4096,128]{1,0:T(8,128)} %bitcast.337, f32[]{:T(128)} %constant.16.clone.1), kind=kCustom, calls=%fused_computation.20 | custom fusion | flops 524288 | bytes 4194816
  276.2 3.8 convert_bitcast_fusion
  280.1 87.6 %reduce-scatter.2.cloned.1.call-done = f32[512,128]{1,0:T(8,128)} async-done(((f32[16384,128]{1,0:T(8,128)}), f32[512,128]{1,0:T(8,128)}) %reduce-scatter.2.cloned.1.call-update) | async-done | bytes 262160 | tf_op jit(solution)/shard_map/reduce_scatter | solution.py:139
  367.7 1.7 subtract_convert_fusion.1
  369.4 3.6 subtract_convert_fusion
  373.0 56.3 %all-gather.2.cloned.1.call-done = bf16[16384,128]{1,0:T(8,128)(2,1)} async-done(((bf16[512,128]{1,0:T(8,128)(2,1)}), bf16[16384,128]{1,0:T(8,128)(2,1)}) %all-gather.2.cloned.1.call-update) | async-done | bytes 4194320 | tf_op jit(solution)/shard_map/all_gather | solution.py:151
  429.3 4.7 %copy.342 = bf16[32,512,128]{2,1,0:T(8,128)(2,1)} copy(bf16[32,512,128]{2,1,0:T(8,128)(2,1)} %bitcast.285) | data formatting | bytes 8388608
  (184 shorter events, 61.9 us)
Async XLA Ops:
  8.0 1.5 copy-start
  9.5 51.2 %copy-start.8 = (s32[16,128]{1,0:T(8,128)}, s32[16,128]{1,0:T(8,128)S(1)}, u32[]{:S(2)}) copy-start(s32[16,128]{1,0:T(8,128)S(1)} %get-tuple-element.6) | copy-start | bytes 24580
  9.5 51.2 %copy-start.10 = (s32[16,128]{1,0:T(8,128)}, s32[16,128]{1,0:T(8,128)S(1)}, u32[]{:S(2)}) copy-start(s32[16,128]{1,0:T(8,128)S(1)} %get-tuple-element.7) | copy-start | bytes 24580
  9.7 51.1 %copy-start.6 = (s32[16,256]{1,0:T(8,128)}, s32[16,256]{1,0:T(8,128)S(1)}, u32[]{:S(2)}) copy-start(s32[16,256]{1,0:T(8,128)S(1)} %add_select_fusion) | copy-start | bytes 49156
  10.4 58.9 %copy-start.17 = (s32[256,32]{0,1:T(8,128)S(1)}, s32[256,32]{0,1:T(8,128)}, u32[]{:S(2)}) copy-start(s32[256,32]{0,1:T(8,128)} %param.12) | copy-start | bytes 98308
  60.7 30.5 %all-to-all-start = ((bf16[1,16,256,128]{3,2,0,1:T(8,128)(2,1)}), bf16[1,16,256,128]{3,2,0,1:T(8,128)(2,1)S(1)}, u32[]{:S(2)}, u32[]{:S(2)}) async-start(bf16[1,16,256,128]{3,2,0,1:T(8,128)(2,1)} %fusion.26), calls=%async_computation | async-start | bytes 2097152 | tf_op jit(solution)/shard_map/all_to_all | solution.py:108
  68.4 299.3 %reduce-scatter.2.cloned.1.call-start = ((), (), s32[]{:S(2)}) async-start(), calls=%async_computation.3 | async-start | bytes 8650752 | tf_op jit(solution)/shard_map/reduce_scatter | solution.py:139
  69.4 22.8 %copy-start.5 = (bf16[256,128]{1,0:T(8,128)(2,1)S(1)}, bf16[256,128]{1,0:T(8,128)(2,1)}, u32[]{:S(2)}) copy-start(bf16[256,128]{1,0:T(8,128)(2,1)} %param.11) | copy-start | bytes 196612
  91.2 1.0 copy-start.4
  138.0 4.6 %copy-start.12 = (s32[256]{0:T(256)S(1)}, s32[256]{0:T(256)}, u32[]{:S(2)}) copy-start(s32[256]{0:T(256)} %param.13) | copy-start | bytes 3076
  138.1 4.6 %copy-start.16 = (bf16[1304,1024]{1,0:T(8,128)(2,1)S(1)}, bf16[1304,1024]{1,0:T(8,128)(2,1)}, u32[]{:S(2)}) copy-start(bf16[1304,1024]{1,0:T(8,128)(2,1)} %param.19) | copy-start | bytes 8011780
  138.1 4.6 %copy-start.19 = (f32[1024]{0:T(1024)S(1)}, f32[1024]{0:T(1024)}, u32[]{:S(2)}) copy-start(f32[1024]{0:T(1024)} %param.21) | copy-start | bytes 12292
  143.9 4.9 %copy-start.14 = (pred[49]{0:T(512)(128)(4,1)S(1)}, pred[49]{0:T(512)(128)(4,1)}, u32[]{:S(2)}) copy-start(pred[49]{0:T(512)(128)(4,1)} %constant.17.clone.1) | copy-start | bytes 151
  195.1 7.5 %copy-start.18 = (s32[256,32]{0,1:T(8,128)S(1)}, s32[256,32]{0,1:T(8,128)}, u32[]{:S(2)}) copy-start(s32[256,32]{0,1:T(8,128)} %param.12) | copy-start | bytes 98308
  199.6 1.8 copy-start.3
  208.9 10.3 %copy-start.13 = (s32[2]{0:T(128)S(1)}, s32[2]{0:T(128)}, u32[]{:S(2)}) copy-start(s32[2]{0:T(128)} %constant.154) | copy-start | bytes 28
  208.9 10.5 %copy-start.15 = (s32[2]{0:T(128)S(1)}, s32[2]{0:T(128)}, u32[]{:S(2)}) copy-start(s32[2]{0:T(128)} %constant.157) | copy-start | bytes 28
  208.9 40.0 %copy-start.7 = (s32[16,256]{1,0:T(8,128)S(1)}, s32[16,256]{1,0:T(8,128)}, u32[]{:S(2)}) copy-start(s32[16,256]{1,0:T(8,128)} %copy-done.6) | copy-start | bytes 49156
  208.9 40.0 %copy-start.9 = (s32[16,128]{1,0:T(8,128)S(1)}, s32[16,128]{1,0:T(8,128)}, u32[]{:S(2)}) copy-start(s32[16,128]{1,0:T(8,128)} %copy-done.8) | copy-start | bytes 24580
  208.9 40.0 %copy-start.11 = (s32[16,128]{1,0:T(8,128)S(1)}, s32[16,128]{1,0:T(8,128)}, u32[]{:S(2)}) copy-start(s32[16,128]{1,0:T(8,128)} %copy-done.10) | copy-start | bytes 24580
  212.1 36.7 %all-to-all-start.1 = ((bf16[16,1,256,128]{3,2,1,0:T(8,128)(2,1)}), bf16[16,1,256,128]{3,2,1,0:T(8,128)(2,1)S(1)}, u32[]{:S(2)}, u32[]{:S(2)}) async-start(bf16[16,1,256,128]{3,2,1,0:T(8,128)(2,1)} %copy.228), calls=%async_computation.2 | async-start | bytes 2097152 | tf_op jit(solution)/shard_map/all_to_all | solution.py:155
  218.9 150.5 %all-reduce.50.cloned.1.call-start = ((), (), s32[]{:S(2)}) async-start(), calls=%async_computation.5 | async-start | bytes 4194304 | tf_op jit(solution)/shard_map/psum | solution.py:167
  251.2 118.2 %copy-start.2 = (bf16[1,8192,128]{2,1,0:T(8,128)(2,1)S(1)}, bf16[1,8192,128]{2,1,0:T(8,128)(2,1)}, u32[]{:S(2)}) copy-start(bf16[1,8192,128]{2,1,0:T(8,128)(2,1)} %param.15) | copy-start | bytes 6291460
  280.0 149.2 %all-gather.2.cloned.1.call-start = ((), (), s32[]{:S(2)}) async-start(), calls=%async_computation.4 | async-start | bytes 4325376 | tf_op jit(solution)/shard_map/all_gather | solution.py:151
  369.4 64.6 %copy-start.1 = (s32[16,32]{1,0:T(8,128)S(1)}, s32[16,32]{1,0:T(8,128)}, u32[]{:S(2)}) copy-start(s32[16,32]{1,0:T(8,128)} %param.16) | copy-start | bytes 6148
Sparse Core Ops, SparseCore 0:
  209.0 158.5 reduce-scatter.1
  371.1 58.0 all-gather.1
Sparse Core Ops, SparseCore 1:
  280.1 74.3 all-reduce.49
where the time goes:
time: 446 us; the launch traced here: 442 us
  waiting for transfers between devices  187 us (42%)
  local copies, waits for them, and re-layouts  147 us (33%)
  other arithmetic  45.6 us (10%)
  matrix products  30.3 us (7%)
  between operations  16.4 us (4%)
  starting transfers between devices  15 us (3%)
    reduce_scatter x1, waiting for transfers between devices, shards(): lax.psum_scatter(small_local.reshape(small_count * small_rows, embed_widt...  87.6 us
    all_gather x1, waiting for transfers between devices, shards(): lax.all_gather(updated, ('rep', 'shard'), axis=0, tiled=True)  56.3 us
    gather x2, local copies, waits for them, and re-layouts, take_rows(): return table_one[row_list]  48 us
    unnamed x89, local copies, waits for them, and re-layouts  38.9 us
    slice x48, local copies, waits for them, and re-layouts, lower_pairs(): pieces = [gram_matrix[:, index, :index] for index in range(1, vec_count)]  35.8 us
    all_to_all x1, waiting for transfers between devices, shards(): lax.all_to_all(jnp.transpose(large_grad_part, (1, 0, 2))[:, None], 'shard...  29.3 us
    unnamed x6, other arithmetic  26 us
    all_to_all x1, waiting for transfers between devices, shards(): lax.all_to_all(expanded, 'shard', split_axis=1, concat_axis=0, tiled=True)  13.8 us
  transfers between devices with their start and end apart: 5, of which 4 were waited for; matrix products, arithmetic and copies ran while one was open for 11% of the time, Pallas kernels for 0%

commit v1 on v0

v1 whole, which is shorter than its diff:
```python
import functools

import jax
import jax.numpy as jnp
from jax import lax
from jax.experimental import pallas as pl
from jax.experimental.pallas import tpu as pltpu
from jax.sharding import PartitionSpec as P

step_size = 32.0
LANES = 128
VMEM_LIMIT = 60 * 1024 * 1024
f32 = jnp.float32
bf16 = jnp.bfloat16


def whole(space):
    return pl.BlockSpec(memory_space=space)


def iota(shape, axis):
    return lax.broadcasted_iota(jnp.int32, shape, axis)


def members_of(ends, slots):
    span = ends.shape[-1]
    starts = jnp.where(iota((1, span), 1) == 0, 0, pltpu.roll(ends, 1, 1))
    places = iota((slots, span), 0)
    return ((places >= starts) & (places < ends)).astype(f32).astype(bf16)


def pool_kernel(rows_ref, count_ref, ends_ref, table_ref, out_ref, wide, picked):
    owners, slots = rows_ref.shape
    wide[...] = table_ref[...].astype(f32)
    picked[...] = jnp.zeros_like(picked)

    def owner(d, carry):
        def group(g, c):
            base = pl.multiple_of(g * 8, 8)
            parts = [wide[pl.ds(rows_ref[d, base + u], 1), :] for u in range(8)]
            picked[pl.ds(base, 8), :] = jnp.concatenate(parts, axis=0)
            return c

        lax.fori_loop(0, (count_ref[d] + 7) // 8, group, 0)
        members = members_of(ends_ref[pl.ds(d, 1), :], slots)
        pooled = lax.dot_general(
            members, picked[...].astype(bf16), (((0,), (0,)), ((), ())),
            preferred_element_type=f32,
        )
        out_ref[d] = pooled.astype(bf16)
        return carry

    lax.fori_loop(0, owners, owner, 0)


def pool(rows, counts, ends, table):
    owners, slots = rows.shape
    width = table.shape[1]
    return pl.pallas_call(
        pool_kernel,
        out_shape=jax.ShapeDtypeStruct((owners, ends.shape[1], width), bf16),
        in_specs=[whole(pltpu.SMEM), whole(pltpu.SMEM), whole(pltpu.VMEM), whole(pltpu.VMEM)],
        out_specs=whole(pltpu.VMEM),
        scratch_shapes=[
            pltpu.VMEM(table.shape, f32),
            pltpu.VMEM((slots, width), f32),
        ],
        compiler_params=pltpu.CompilerParams(vmem_limit_bytes=VMEM_LIMIT),
        name="pool",
    )(rows, counts, ends, table)


def scatter_kernel(rows_ref, count_ref, ends_ref, fold_ref, table_ref, out_ref, spread, *sums):
    owners, slots = rows_ref.shape
    lanes_of = len(sums)
    for total in sums:
        total[...] = jnp.zeros_like(total)

    def owner(d, carry):
        members = members_of(ends_ref[pl.ds(d, 1), :], slots)
        spread[...] = jnp.dot(members, fold_ref[d], preferred_element_type=f32)

        def group(g, c):
            base = pl.multiple_of(g * 8, 8)
            block = spread[pl.ds(base, 8), :]
            for u in range(0, 8, lanes_of):
                spots = [rows_ref[d, base + u + v] for v in range(lanes_of)]
                news = [
                    sums[v][pl.ds(spots[v], 1), :] + block[u + v : u + v + 1]
                    for v in range(lanes_of)
                ]
                for v in range(lanes_of):
                    sums[v][pl.ds(spots[v], 1), :] = news[v]
            return c

        lax.fori_loop(0, (count_ref[d] + 7) // 8, group, 0)
        return carry

    lax.fori_loop(0, owners, owner, 0)
    step = 256

    def finish(g, c):
        at = pl.ds(pl.multiple_of(g * step, step), step)
        total = sums[0][at, :]
        for other in sums[1:]:
            total = total + other[at, :]
        out_ref[at, :] = (table_ref[at, :].astype(f32) - step_size * total).astype(bf16)
        return c

    lax.fori_loop(0, table_ref.shape[0] // step, finish, 0)


def scatter(rows, counts, ends, fold, table):
    slots = rows.shape[1]
    return pl.pallas_call(
        scatter_kernel,
        out_shape=jax.ShapeDtypeStruct(table.shape, bf16),
        in_specs=[whole(pltpu.SMEM), whole(pltpu.SMEM)] + [whole(pltpu.VMEM)] * 3,
        out_specs=whole(pltpu.VMEM),
        scratch_shapes=[pltpu.VMEM((slots, table.shape[1]), f32)]
        + [pltpu.VMEM(table.shape, f32)] * 4,
        compiler_params=pltpu.CompilerParams(vmem_limit_bytes=VMEM_LIMIT),
        name="scatter",
    )(rows, counts, ends, fold, table)


def small_kernel(part_rows, first_ref, ids_ref, grads_ref, table_ref, out_ref):
    senders, batch = ids_ref.shape
    rows = iota((part_rows, batch), 0) + first_ref[0]
    total = jnp.zeros(out_ref.shape, f32)

    def one(s, total):
        hot = (rows == ids_ref[pl.ds(s, 1), :]).astype(f32).astype(bf16)
        return total + jnp.dot(hot, grads_ref[s], preferred_element_type=f32)

    total = lax.fori_loop(0, senders, one, total)
    out_ref[...] = (table_ref[...].astype(f32) - step_size * total).astype(bf16)


def small_update(first, ids, grads, rows):
    return pl.pallas_call(
        functools.partial(small_kernel, rows.shape[0]),
        out_shape=jax.ShapeDtypeStruct(rows.shape, bf16),
        in_specs=[whole(pltpu.SMEM)] + [whole(pltpu.VMEM)] * 3,
        out_specs=whole(pltpu.VMEM),
        compiler_params=pltpu.CompilerParams(vmem_limit_bytes=VMEM_LIMIT),
        name="small_update",
    )(first, ids, grads, rows)


def spans_of(vec_count):
    return [(i, i * (i - 1) // 2) for i in range(1, vec_count)]


def top_kernel(
    vec_count, pad, sizes_ref, dense_ref, ids_ref, labels_ref, tables_ref, large_ref,
    w_ref, wd_ref, bias_ref, wout_ref, small_out, fold_out, vecs, gram, pairs, spread,
):
    batch, width = dense_ref.shape
    small_count, small_rows = tables_ref.shape[0], tables_ref.shape[1]
    feats, bag_span = large_ref.shape[0], large_ref.shape[1]
    pair_pad = pairs.shape[1]
    scale = width ** (-0.5)
    spans = spans_of(vec_count)

    def rows_of(i):
        return pl.ds(i, batch, stride=pad)

    vecs[rows_of(0), :] = dense_ref[...].astype(f32)
    rows = iota((batch, small_rows), 1)
    for t in range(small_count):
        hot = (ids_ref[:, t : t + 1] == rows).astype(f32).astype(bf16)
        vecs[rows_of(1 + t), :] = jnp.dot(hot, tables_ref[t], preferred_element_type=f32)
    sample = iota((batch, bag_span), 0)
    bag = iota((batch, bag_span), 1) * batch
    for f in range(feats):
        reach = sample * sizes_ref[f]
        hot = ((reach >= bag) & (reach < bag + batch)).astype(f32).astype(bf16)
        vecs[rows_of(1 + small_count + f), :] = jnp.dot(
            hot, large_ref[f], preferred_element_type=f32
        )
    for i in range(vec_count, pad):
        vecs[rows_of(i), :] = jnp.zeros((batch, width), f32)

    unroll = 8

    def gram_step(g, c):
        for u in range(unroll):
            at = pl.ds(pl.multiple_of((g * unroll + u) * pad, 8), pad)
            own = vecs[at, :].astype(bf16)
            gram[at, 0:pad] = lax.dot_general(
                own, own, (((1,), (1,)), ((), ())), preferred_element_type=f32
            )
        return c

    lax.fori_loop(0, batch // unroll, gram_step, 0)

    lane = iota((1, LANES), 1)
    chunk = 64
    for start in range(0, batch, chunk):
        tile = jnp.zeros((chunk, LANES), f32)
        at_tile = 0
        for i, off in spans:
            piece = gram[pl.ds(start * pad + i, chunk, stride=pad), :]
            turn = off % LANES
            if turn:
                piece = pltpu.roll(piece, turn, 1)
            low = off - at_tile * LANES
            tile = jnp.where((lane >= low) & (lane < low + i), piece, tile)
            if low + i >= LANES:
                pairs[start : start + chunk, at_tile * LANES : (at_tile + 1) * LANES] = (
                    tile * scale
                ).astype(bf16)
                at_tile += 1
                rest = low + i - LANES
                tile = jnp.where(lane < rest, piece, jnp.zeros_like(piece))
        if at_tile * LANES < pair_pad:
            pairs[start : start + chunk, at_tile * LANES : pair_pad] = (tile * scale).astype(bf16)

    block = 128
    for start in range(0, batch, block):
        at = slice(start, start + block)
        preact = (
            jnp.dot(pairs[at, :], w_ref[0:pair_pad, :], preferred_element_type=f32)
            + jnp.dot(dense_ref[at, :], wd_ref[...], preferred_element_type=f32)
            + bias_ref[...]
        )
        squash = jax.nn.sigmoid(preact)
        logits = jnp.sum(preact * squash * wout_ref[...], axis=1, keepdims=True)
        grad = jax.nn.sigmoid(logits) - labels_ref[at, :].astype(f32)
        pre_grad = (
            grad * wout_ref[...] * (squash * (1.0 + preact * (1.0 - squash)))
        ).astype(bf16)
        for q in range(0, pair_pad, LANES):
            spread[at, q : q + LANES] = lax.dot_general(
                pre_grad, w_ref[q : q + LANES, :], (((1,), (1,)), ((), ())),
                preferred_element_type=f32,
            ) * scale

    gram[rows_of(0), :] = jnp.zeros((batch, LANES), f32)
    for i in range(vec_count, pad):
        gram[rows_of(i), :] = jnp.zeros((batch, LANES), f32)
    for start in range(0, batch, chunk):
        for i, off in spans:
            first = off // LANES
            low = off - first * LANES
            here = spread[start : start + chunk, first * LANES : (first + 1) * LANES]
            if low + i > LANES:
                after = spread[start : start + chunk, (first + 1) * LANES : (first + 2) * LANES]
                here = jnp.where(lane >= low, here, after)
            if low:
                here = pltpu.roll(here, LANES - low, 1)
            gram[pl.ds(start * pad + i, chunk, stride=pad), :] = jnp.where(lane < i, here, 0.0)

    def back_step(g, c):
        for u in range(unroll):
            at = pl.ds(pl.multiple_of((g * unroll + u) * pad, 8), pad)
            lower = gram[at, :]
            both = lower[:, 0:pad] + jnp.transpose(lower)[0:pad, :]
            vecs[at, :] = jnp.dot(
                both.astype(bf16), vecs[at, :].astype(bf16), preferred_element_type=f32
            )
        return c

    lax.fori_loop(0, batch // unroll, back_step, 0)

    for t in range(small_count):
        small_out[t] = vecs[rows_of(1 + t), :].astype(bf16)
    sample_lane = iota((bag_span, batch), 1)
    bag_row = iota((bag_span, batch), 0) * batch
    for f in range(feats):
        reach = sample_lane * sizes_ref[f]
        hot = ((reach >= bag_row) & (reach < bag_row + batch)).astype(f32).astype(bf16)
        fold_out[f] = jnp.dot(
            hot, vecs[rows_of(1 + small_count + f), :].astype(bf16), preferred_element_type=f32
        ).astype(bf16)


def top(sizes, dense, ids, labels, tables, large, w_first, bias, wout):
    batch, width = dense.shape
    small_count, feats, bag_span = tables.shape[0], large.shape[0], large.shape[1]
    vec_count = 1 + small_count + feats
    pad = -(-vec_count // 8) * 8
    pair_count = vec_count * (vec_count - 1) // 2
    pair_pad = -(-pair_count // LANES) * LANES
    return pl.pallas_call(
        functools.partial(top_kernel, vec_count, pad),
        out_shape=(
            jax.ShapeDtypeStruct((small_count, batch, width), bf16),
            jax.ShapeDtypeStruct((feats, bag_span, width), bf16),
        ),
        in_specs=[whole(pltpu.SMEM)] + [whole(pltpu.VMEM)] * 9,
        out_specs=(whole(pltpu.VMEM), whole(pltpu.VMEM)),
        scratch_shapes=[
            pltpu.VMEM((batch * pad, width), f32),
            pltpu.VMEM((batch * pad, LANES), f32),
            pltpu.VMEM((batch, pair_pad), bf16),
            pltpu.VMEM((batch, pair_pad), f32),
        ],
        compiler_params=pltpu.CompilerParams(vmem_limit_bytes=VMEM_LIMIT),
        name="top",
    )(
        sizes, dense, ids, labels[:, None], tables, large, w_first, w_first[pair_count:],
        bias[None, :], wout[None, :],
    )


def shards(
    dense, small_ids, labels, small_tables, large_tables, batch_sizes, bag_ends,
    owner_row_index, w_first, b_first, w_out,
):
    groups = lax.axis_size("shard")
    copies = lax.axis_size("rep")
    replica = lax.axis_index("rep")
    member = lax.axis_index("shard")
    devices = groups * copies
    index = replica * groups + member
    small_count, small_rows, width = small_tables.shape
    batch = dense.shape[0]
    per_table = devices // small_count

    ids_by_table = jnp.transpose(small_ids)
    sent_ids = jnp.repeat(ids_by_table, per_table, axis=0)
    all_ids = lax.all_to_all(sent_ids, ("rep", "shard"), split_axis=0, concat_axis=0, tiled=True)

    ends, rows, table = bag_ends[0], owner_row_index[0], large_tables[0]
    counts = ends[:, -1]
    first = replica * groups

    def mine(x):
        return lax.dynamic_slice_in_dim(x, first, groups, 0)

    pooled = pool(mine(rows), mine(counts), mine(ends), table)
    large = lax.all_to_all(pooled, "shard", split_axis=0, concat_axis=0, tiled=True)
    sizes = lax.dynamic_slice_in_dim(batch_sizes, index, 1, 1)[:, 0]
    small_grads, fold = top(
        sizes, dense, small_ids, labels, small_tables, large, w_first, b_first, w_out
    )
    fold_back = lax.all_to_all(fold, "shard", split_axis=0, concat_axis=0, tiled=True)
    fold_all = lax.all_gather(fold_back, "rep", axis=0, tiled=True)
    sent = jnp.repeat(small_grads, per_table, axis=0)
    arrived = lax.all_to_all(sent, ("rep", "shard"), split_axis=0, concat_axis=0, tiled=True)
    part_rows = small_count * small_rows // devices
    flat = small_tables.reshape(small_count * small_rows, width)
    own = lax.dynamic_slice_in_dim(flat, index * part_rows, part_rows, 0)
    first_row = (lax.rem(index, per_table) * part_rows)[None].astype(jnp.int32)
    updated = small_update(first_row, all_ids, arrived, own)
    small_new = lax.all_gather(updated, ("rep", "shard"), axis=0, tiled=True).reshape(
        small_count, small_rows, width
    )
    large_new = scatter(rows, counts, ends, fold_all, table)
    return small_new, large_new[None]


def solution(mesh):
    both = ("rep", "shard")
    placed = (
        P(both, None), P(both, None), P(both), P(), P("shard", None, None), P(),
        P("shard", None, None), P("shard", None, None), P(), P(), P(),
    )
    return jax.shard_map(
        shards, mesh=mesh, in_specs=placed, out_specs=(P(), P("shard", None, None)), check_vma=False
    )
```

time: 446 us -> 243 us (0.54)
  local copies, waits for them, and re-layouts: 147 us -> 17.6 us
  waiting for transfers between devices: 187 us -> 94.2 us
  Pallas kernels: 0 us -> 78.8 us
  other arithmetic: 45.6 us -> 0 us
  matrix products: 30.3 us -> 0 us
  blocking collectives: 0 us -> 20.3 us
    reduce_scatter x1 -> x0, waiting for transfers between devices: 87.6 us -> none  [shards(): lax.psum_scatter(small_local.reshape(small_count * small_rows, embed_widt...]
    pallas_call x0 -> x4, Pallas kernels: none -> 78.8 us  [the longest x1 28.8 us: top(): pl.pallas_call(functools.partial(top_kernel, vec_count, pad), out_shape=(...]
    gather x2 -> x0, local copies, waits for them, and re-layouts: 48 us -> none  [take_rows(): return table_one[row_list]]
    slice x97 -> x2, local copies, waits for them, and re-layouts: 42.2 us -> 3.15 us  [the longest x1 1.66 us: top(): w_first[pair_count:]]
    unnamed x89 -> x13, local copies, waits for them, and re-layouts: 38.9 us -> 7.37 us
    dot_general x8 -> x0, matrix products: 30.3 us -> none  [the longest x1 8.1 us: shards(): jnp.einsum('btr,tre->bte', small_hot, small_tables, preferred_element_typ...]
    unnamed x6 -> x0, other arithmetic: 26 us -> none
    all_gather x1, waiting for transfers between devices: 56.3 us -> 32.7 us  [shards(): lax.all_gather(updated, ('rep', 'shard'), axis=0, tiled=True)]
  transfers between devices with their start and end apart: 5 -> 5, of which waited for: 4 -> 3; matrix products, arithmetic and copies ran while one was open for 11% -> 3% of each run, Pallas kernels for 0% -> 27%
where the time goes in v1:
time: 243 us; the launch traced here: 242 us
  waiting for transfers between devices  94.2 us (39%)
  Pallas kernels  78.8 us (32%)
  blocking collectives  20.3 us (8%)
  local copies, waits for them, and re-layouts  17.6 us (7%)
  starting transfers between devices  16.8 us (7%)
  between operations  14.1 us (6%)
    all_to_all x1, waiting for transfers between devices, shards(): lax.all_to_all(sent, ('rep', 'shard'), split_axis=0, concat_axis=0, tiled...  47.2 us
    all_gather x1, waiting for transfers between devices, shards(): lax.all_gather(updated, ('rep', 'shard'), axis=0, tiled=True)  32.7 us
    pallas_call x1, Pallas kernels, top(): pl.pallas_call(functools.partial(top_kernel, vec_count, pad), out_shape=(...  28.8 us
    pallas_call x1, Pallas kernels, scatter(): pl.pallas_call(scatter_kernel, out_shape=jax.ShapeDtypeStruct(table.shape...  26.1 us
    all_to_all x1, blocking collectives, shards(): lax.all_to_all(fold, 'shard', split_axis=0, concat_axis=0, tiled=True)  20.3 us
    pallas_call x1, Pallas kernels, pool(): pl.pallas_call(pool_kernel, out_shape=jax.ShapeDtypeStruct((owners, ends....  13.7 us
    all_to_all x1, waiting for transfers between devices, shards(): lax.all_to_all(pooled, 'shard', split_axis=0, concat_axis=0, tiled=True)  13.6 us
    pallas_call x1, Pallas kernels, small_update(): pl.pallas_call(functools.partial(small_kernel, rows.shape[0]), out_shape=...  10.2 us
  transfers between devices with their start and end apart: 5, of which 3 were waited for; matrix products, arithmetic and copies ran while one was open for 3% of the time, Pallas kernels for 27%

profile of v1, /device:TPU:0, one launch (start us, length us, event | category | flops | bytes accessed | tf_op | source)
XLA Modules:
  0.0 241.8 jit_solution(17930027151129407202)
XLA Ops:
  7.2 0.0 copy-start
  7.2 0.0 copy-start.3
  7.2 0.0 copy-start.4
  7.2 1.3 dynamic-slice_bitcast_fusion.1.ends_ref
  8.5 1.3 dynamic-slice_bitcast_fusion.rows_ref
  9.8 1.5 slice_reduce_fusion
  11.3 0.7 dynamic-slice_reduce_fusion.count_ref
  12.0 13.7 %pool.1 = bf16[16,128,128]{2,1,0:T(8,128)(2,1)} custom-call(s32[16,256]{1,0:T(8,128)} %dynamic-slice_bitcast_fusion.rows_ref, s32[16]{0:T(128)} %dynamic-slice_reduce_fusion.count_ref, s32[16,128]{1,0:T(8,128)} %dynamic-slice_bitcast_fusion.1.ends_ref, bf16[8192,128]{1,0:T(8,128)(2,1)} %bitcast.17), custom_call_target="tpu_custom_call" | custom-call | tf_op jit(solution)/shard_map/pool/pallas_call | solution.py:59
  25.7 9.5 %all-to-all-start.1 = ((bf16[16,128,128]{2,1,0:T(8,128)(2,1)}), bf16[16,128,128]{2,1,0:T(8,128)(2,1)S(1)}, u32[]{:S(2)}, u32[]{:S(2)}) async-start(bf16[16,128,128]{2,1,0:T(8,128)(2,1)} %pool.1), calls=%async_computation.1 | async-start | bytes 1048576 | tf_op jit(solution)/shard_map/all_to_all | solution.py:334
  35.2 0.0 copy-done.3
  35.2 0.6 all_to_all.16
  35.8 13.6 %all-to-all-done.1.large_ref = bf16[16,128,128]{2,1,0:T(8,128)(2,1)S(1)} async-done(((bf16[16,128,128]{2,1,0:T(8,128)(2,1)}), bf16[16,128,128]{2,1,0:T(8,128)(2,1)S(1)}, u32[]{:S(2)}, u32[]{:S(2)}) %all-to-all-start.1) | async-done | bytes 524320 | tf_op jit(solution)/shard_map/all_to_all | solution.py:334
  49.4 0.0 copy-start.2
  49.4 3.1 %all-to-all-start = ((s32[32,1,256]{2,1,0:T(1,128)}), s32[32,1,256]{2,1,0:T(1,128)S(1)}, u32[]{:S(2)}, u32[]{:S(2)}) async-start(s32[32,1,256]{2,1,0:T(1,128)} %all_to_all.16), calls=%async_computation | async-start | bytes 65536 | tf_op jit(solution)/shard_map/all_to_all | solution.py:324
  52.6 0.8 copy.16.ids_ref
  53.4 0.0 copy-done.4
  53.4 0.8 copy.17.labels_ref
  54.2 1.7 slice.7.wd_ref
  55.8 0.0 copy-done
  55.8 0.8 dynamic-slice_reduce_fusion.1.sizes_ref
  56.6 0.0 copy-done.2
  56.6 28.8 %top.1 = (bf16[32,256,128]{2,1,0:T(8,128)(2,1)}, bf16[16,128,128]{2,1,0:T(8,128)(2,1)}) custom-call(s32[16]{0:T(128)} %dynamic-slice_reduce_fusion.1.sizes_ref, bf16[256,128]{1,0:T(8,128)(2,1)} %dense_ref.1, s32[256,32]{1,0:T(8,128)} %copy.16.ids_ref, s32[256,1]{1,0:T(8,128)} %copy.17.labels_ref, bf16[32,512,128]{2,1,0:T(8,128)(2,1)} %tables_ref.1, ...), custom_call_target="tpu_custom_call" | custom-call | tf_op jit(solution)/shard_map/top/pallas_call | solution.py:286
  85.4 0.0 all-to-all-done
  85.4 20.3 %all_to_all.26 = bf16[16,128,128]{2,1,0:T(8,128)(2,1)} all-to-all(bf16[16,128,128]{2,1,0:T(8,128)(2,1)} %get-tuple-element.5), channel_id=1, replica_groups=mesh['rep'=2,'shard'=16] {'shard'}, dimensions={0} | all-to-all | bytes 1048576 | tf_op jit(solution)/shard_map/all_to_all | solution.py:339
  105.7 4.1 %all-to-all-start.2 = ((bf16[32,256,128]{2,1,0:T(8,128)(2,1)}), bf16[32,256,128]{2,1,0:T(8,128)(2,1)S(1)}, u32[]{:S(2)}, u32[]{:S(2)}) async-start(bf16[32,256,128]{2,1,0:T(8,128)(2,1)} %get-tuple-element.4), calls=%async_computation.2 | async-start | bytes 4194304 | tf_op jit(solution)/shard_map/all_to_all | solution.py:342
  109.8 0.0 all-gather.5.cloned.1.call-start
  109.9 0.7 all-gather.5.cloned.1.call-update
  110.6 0.0 all-gather.3.cloned.1.call-start
  110.6 1.6 constant_dynamic-slice_fusion.table_ref
  112.2 0.6 copy.20
  112.8 47.2 %all-to-all-done.2.grads_ref = bf16[32,256,128]{2,1,0:T(8,128)(2,1)S(1)} async-done(((bf16[32,256,128]{2,1,0:T(8,128)(2,1)}), bf16[32,256,128]{2,1,0:T(8,128)(2,1)S(1)}, u32[]{:S(2)}, u32[]{:S(2)}) %all-to-all-start.2) | async-done | bytes 2097184 | tf_op jit(solution)/shard_map/all_to_all | solution.py:342
  160.0 0.0 copy-start.1
  160.0 1.3 copy-done.1
  161.3 10.2 %small_update.1 = bf16[512,128]{1,0:T(8,128)(2,1)} custom-call(s32[1]{0:T(128)} %constant.19.clone.1.first_ref, s32[32,256]{1,0:T(8,128)} %bitcast.23, bf16[32,256,128]{2,1,0:T(8,128)(2,1)} %copy-done.1, bf16[512,128]{1,0:T(8,128)(2,1)} %constant_dynamic-slice_fusion.table_ref), custom_call_target="tpu_custom_call" | custom-call | tf_op jit(solution)/shard_map/small_update/pallas_call | solution.py:141
  171.5 0.0 all-gather.3.cloned.1.call-update
  171.5 0.0 all-gather.5.cloned.1.call-done.fold_ref
  171.6 26.1 %scatter.1 = bf16[8192,128]{1,0:T(8,128)(2,1)} custom-call(s32[32,256]{1,0:T(8,128)} %bitcast.26, s32[32]{0:T(128)} %get-tuple-element.6.count_ref, s32[32,128]{1,0:T(8,128)} %bitcast.25, bf16[32,128,128]{2,1,0:T(8,128)(2,1)} %all-gather.5.cloned.1.call-done.fold_ref, bf16[8192,128]{1,0:T(8,128)(2,1)} %bitcast.18), custom_call_target="tpu_custom_call" | custom-call | tf_op jit(solution)/shard_map/scatter/pallas_call | solution.py:115
  197.6 32.7 %all-gather.3.cloned.1.call-done = bf16[16384,128]{1,0:T(8,128)(2,1)} async-done(((bf16[512,128]{1,0:T(8,128)(2,1)}), bf16[16384,128]{1,0:T(8,128)(2,1)}) %all-gather.3.cloned.1.call-update) | async-done | bytes 4194320 | tf_op jit(solution)/shard_map/all_gather | solution.py:348
  230.3 4.7 %copy.22 = bf16[32,512,128]{2,1,0:T(8,128)(2,1)} copy(bf16[32,512,128]{2,1,0:T(8,128)(2,1)} %bitcast.20) | data formatting | bytes 8388608
Async XLA Ops:
  7.2 48.7 %copy-start = (s32[16,32]{1,0:T(8,128)S(1)}, s32[16,32]{1,0:T(8,128)}, u32[]{:S(2)}) copy-start(s32[16,32]{1,0:T(8,128)} %param.16) | copy-start | bytes 6148
  7.2 28.0 %copy-start.3 = (s32[256,32]{0,1:T(8,128)S(1)}, s32[256,32]{0,1:T(8,128)}, u32[]{:S(2)}) copy-start(s32[256,32]{0,1:T(8,128)} %param.12) | copy-start | bytes 98308
  7.2 46.2 %copy-start.4 = (s32[256]{0:T(256)S(1)}, s32[256]{0:T(256)}, u32[]{:S(2)}) copy-start(s32[256]{0:T(256)} %param.13) | copy-start | bytes 3076
  25.7 23.8 %all-to-all-start.1 = ((bf16[16,128,128]{2,1,0:T(8,128)(2,1)}), bf16[16,128,128]{2,1,0:T(8,128)(2,1)S(1)}, u32[]{:S(2)}, u32[]{:S(2)}) async-start(bf16[16,128,128]{2,1,0:T(8,128)(2,1)} %pool.1), calls=%async_computation.1 | async-start | bytes 1048576 | tf_op jit(solution)/shard_map/all_to_all | solution.py:334
  49.4 7.2 %copy-start.2 = (bf16[16,128,128]{2,1,0:T(8,128)(2,1)}, bf16[16,128,128]{2,1,0:T(8,128)(2,1)S(1)}, u32[]{:S(2)}) copy-start(bf16[16,128,128]{2,1,0:T(8,128)(2,1)S(1)} %all-to-all-done.1.large_ref) | copy-start | bytes 1572868
  49.4 36.0 %all-to-all-start = ((s32[32,1,256]{2,1,0:T(1,128)}), s32[32,1,256]{2,1,0:T(1,128)S(1)}, u32[]{:S(2)}, u32[]{:S(2)}) async-start(s32[32,1,256]{2,1,0:T(1,128)} %all_to_all.16), calls=%async_computation | async-start | bytes 65536 | tf_op jit(solution)/shard_map/all_to_all | solution.py:324
  105.7 54.2 %all-to-all-start.2 = ((bf16[32,256,128]{2,1,0:T(8,128)(2,1)}), bf16[32,256,128]{2,1,0:T(8,128)(2,1)S(1)}, u32[]{:S(2)}, u32[]{:S(2)}) async-start(bf16[32,256,128]{2,1,0:T(8,128)(2,1)} %get-tuple-element.4), calls=%async_computation.2 | async-start | bytes 4194304 | tf_op jit(solution)/shard_map/all_to_all | solution.py:342
  109.8 61.7 %all-gather.5.cloned.1.call-start = ((), (), s32[]{:S(2)}) async-start(), calls=%async_computation.5 | async-start | bytes 1572864 | tf_op jit(solution)/shard_map/all_gather | solution.py:340
  110.6 119.7 %all-gather.3.cloned.1.call-start = ((), (), s32[]{:S(2)}) async-start(), calls=%async_computation.4 | async-start | bytes 4325376 | tf_op jit(solution)/shard_map/all_gather | solution.py:348
  160.0 1.3 copy-start.1
Sparse Core Ops, SparseCore 0:
  112.2 29.1 all-gather.4
  171.7 58.5 all-gather.2

commit v2 on v1

--- a/solution.py
+++ b/solution.py
@@ -29,37 +29,42 @@
     return ((places >= starts) & (places < ends)).astype(f32).astype(bf16)
 
 
-def pool_kernel(rows_ref, count_ref, ends_ref, table_ref, out_ref, wide, picked):
-    owners, slots = rows_ref.shape
+def pool_kernel(first_ref, rows_ref, count_ref, ends_ref, table_ref, out_ref, wide, picked):
+    slots = rows_ref.shape[1]
+    owners = out_ref.shape[0]
+    last = count_ref.shape[1] - 1
+    first = first_ref[0]
     wide[...] = table_ref[...].astype(f32)
     picked[...] = jnp.zeros_like(picked)
 
-    def owner(d, carry):
+    def owner(o, carry):
+        d = o + first
+
         def group(g, c):
             base = pl.multiple_of(g * 8, 8)
             parts = [wide[pl.ds(rows_ref[d, base + u], 1), :] for u in range(8)]
             picked[pl.ds(base, 8), :] = jnp.concatenate(parts, axis=0)
             return c
 
-        lax.fori_loop(0, (count_ref[d] + 7) // 8, group, 0)
+        lax.fori_loop(0, (count_ref[d, last] + 7) // 8, group, 0)
         members = members_of(ends_ref[pl.ds(d, 1), :], slots)
         pooled = lax.dot_general(
             members, picked[...].astype(bf16), (((0,), (0,)), ((), ())),
             preferred_element_type=f32,
         )
-        out_ref[d] = pooled.astype(bf16)
+        out_ref[o] = pooled.astype(bf16)
         return carry
 
     lax.fori_loop(0, owners, owner, 0)
 
 
-def pool(rows, counts, ends, table):
-    owners, slots = rows.shape
+def pool(first, owners, rows, ends, table):
+    slots = rows.shape[1]
     width = table.shape[1]
     return pl.pallas_call(
         pool_kernel,
         out_shape=jax.ShapeDtypeStruct((owners, ends.shape[1], width), bf16),
-        in_specs=[whole(pltpu.SMEM), whole(pltpu.SMEM), whole(pltpu.VMEM), whole(pltpu.VMEM)],
+        in_specs=[whole(pltpu.SMEM)] * 3 + [whole(pltpu.VMEM)] * 2,
         out_specs=whole(pltpu.VMEM),
         scratch_shapes=[
             pltpu.VMEM(table.shape, f32),
@@ -67,11 +72,12 @@
         ],
         compiler_params=pltpu.CompilerParams(vmem_limit_bytes=VMEM_LIMIT),
         name="pool",
-    )(rows, counts, ends, table)
+    )(first, rows, ends, ends, table)
 
 
 def scatter_kernel(rows_ref, count_ref, ends_ref, fold_ref, table_ref, out_ref, spread, *sums):
     owners, slots = rows_ref.shape
+    last = count_ref.shape[1] - 1
     lanes_of = len(sums)
     for total in sums:
         total[...] = jnp.zeros_like(total)
@@ -93,7 +99,7 @@
                     sums[v][pl.ds(spots[v], 1), :] = news[v]
             return c
 
-        lax.fori_loop(0, (count_ref[d] + 7) // 8, group, 0)
+        lax.fori_loop(0, (count_ref[d, last] + 7) // 8, group, 0)
         return carry
 
     lax.fori_loop(0, owners, owner, 0)
@@ -110,7 +116,7 @@
     lax.fori_loop(0, table_ref.shape[0] // step, finish, 0)
 
 
-def scatter(rows, counts, ends, fold, table):
+def scatter(rows, ends, fold, table):
     slots = rows.shape[1]
     return pl.pallas_call(
         scatter_kernel,
@@ -120,8 +126,11 @@
         scratch_shapes=[pltpu.VMEM((slots, table.shape[1]), f32)]
         + [pltpu.VMEM(table.shape, f32)] * 4,
         compiler_params=pltpu.CompilerParams(vmem_limit_bytes=VMEM_LIMIT),
+        cost_estimate=pl.CostEstimate(
+            flops=20 * table.size * LANES, bytes_accessed=4 * table.size, transcendentals=0
+        ),
         name="scatter",
-    )(rows, counts, ends, fold, table)
+    )(rows, ends, ends, fold, table)
 
 
 def small_kernel(part_rows, first_ref, ids_ref, grads_ref, table_ref, out_ref):
@@ -153,13 +162,14 @@
 
 
 def top_kernel(
-    vec_count, pad, sizes_ref, dense_ref, ids_ref, labels_ref, tables_ref, large_ref,
-    w_ref, wd_ref, bias_ref, wout_ref, small_out, fold_out, vecs, gram, pairs, spread,
+    vec_count, pad, index_ref, sizes_ref, dense_ref, ids_ref, labels_ref, tables_ref, large_ref,
+    w_ref, bias_ref, wout_ref, small_out, fold_out, vecs, gram, pairs, spread,
 ):
     batch, width = dense_ref.shape
     small_count, small_rows = tables_ref.shape[0], tables_ref.shape[1]
     feats, bag_span = large_ref.shape[0], large_ref.shape[1]
     pair_pad = pairs.shape[1]
+    pair_count = vec_count * (vec_count - 1) // 2
     scale = width ** (-0.5)
     spans = spans_of(vec_count)
 
@@ -174,7 +184,7 @@
     sample = iota((batch, bag_span), 0)
     bag = iota((batch, bag_span), 1) * batch
     for f in range(feats):
-        reach = sample * sizes_ref[f]
+        reach = sample * sizes_ref[f, index_ref[0]]
         hot = ((reach >= bag) & (reach < bag + batch)).astype(f32).astype(bf16)
         vecs[rows_of(1 + small_count + f), :] = jnp.dot(
             hot, large_ref[f], preferred_element_type=f32
@@ -222,7 +232,7 @@
         at = slice(start, start + block)
         preact = (
             jnp.dot(pairs[at, :], w_ref[0:pair_pad, :], preferred_element_type=f32)
-            + jnp.dot(dense_ref[at, :], wd_ref[...], preferred_element_type=f32)
+            + jnp.dot(dense_ref[at, :], w_ref[pair_count : pair_count + width, :], preferred_element_type=f32)
             + bias_ref[...]
         )
         squash = jax.nn.sigmoid(preact)
@@ -269,14 +279,14 @@
     sample_lane = iota((bag_span, batch), 1)
     bag_row = iota((bag_span, batch), 0) * batch
     for f in range(feats):
-        reach = sample_lane * sizes_ref[f]
+        reach = sample_lane * sizes_ref[f, index_ref[0]]
         hot = ((reach >= bag_row) & (reach < bag_row + batch)).astype(f32).astype(bf16)
         fold_out[f] = jnp.dot(
             hot, vecs[rows_of(1 + small_count + f), :].astype(bf16), preferred_element_type=f32
         ).astype(bf16)
 
 
-def top(sizes, dense, ids, labels, tables, large, w_first, bias, wout):
+def top(index, sizes, dense, ids, labels, tables, large, w_first, bias, wout):
     batch, width = dense.shape
     small_count, feats, bag_span = tables.shape[0], large.shape[0], large.shape[1]
     vec_count = 1 + small_count + feats
@@ -289,7 +299,7 @@
             jax.ShapeDtypeStruct((small_count, batch, width), bf16),
             jax.ShapeDtypeStruct((feats, bag_span, width), bf16),
         ),
-        in_specs=[whole(pltpu.SMEM)] + [whole(pltpu.VMEM)] * 9,
+        in_specs=[whole(pltpu.SMEM)] * 2 + [whole(pltpu.VMEM)] * 8,
         out_specs=(whole(pltpu.VMEM), whole(pltpu.VMEM)),
         scratch_shapes=[
             pltpu.VMEM((batch * pad, width), f32),
@@ -300,9 +310,286 @@
         compiler_params=pltpu.CompilerParams(vmem_limit_bytes=VMEM_LIMIT),
         name="top",
     )(
-        sizes, dense, ids, labels[:, None], tables, large, w_first, w_first[pair_count:],
+        index, sizes, dense, ids, labels[:, None], tables, large, w_first,
         bias[None, :], wout[None, :],
     )
+
+
+def greet_all():
+    copies, groups = lax.axis_size("rep"), lax.axis_size("shard")
+    devices = copies * groups
+    index = lax.axis_index("rep") * groups + lax.axis_index("shard")
+    barrier = pltpu.get_barrier_semaphore()
+
+    def greet(k, c):
+        other = lax.rem(index + k, devices)
+        pl.semaphore_signal(
+            barrier, inc=1, device_id={"rep": other // groups, "shard": lax.rem(other, groups)},
+            device_id_type=pl.DeviceIdType.MESH,
+        )
+        return c
+
+    lax.fori_loop(1, devices, greet, 0)
+    pl.semaphore_wait(barrier, devices - 1)
+
+
+def remote(src, dst, send, recv, rep, shard):
+    return pltpu.make_async_remote_copy(
+        src_ref=src, dst_ref=dst, send_sem=send, recv_sem=recv,
+        device_id={"rep": rep, "shard": shard}, device_id_type=pl.DeviceIdType.MESH,
+    )
+
+
+def forward_kernel(
+    pooled_ref, ids_ref, large_out, ids_out, send, recv, id_send, id_recv, own
+):
+    copies, groups = lax.axis_size("rep"), lax.axis_size("shard")
+    devices = copies * groups
+    rep, me = lax.axis_index("rep"), lax.axis_index("shard")
+    index = rep * groups + me
+
+    def block(k):
+        to = lax.rem(me + k, groups)
+        return remote(pooled_ref.at[to], large_out.at[me], send.at[k], recv.at[k], rep, to)
+
+    def ids(k):
+        to = lax.rem(index + k, devices)
+        return remote(
+            ids_ref.at[to], ids_out.at[index], id_send.at[k], id_recv.at[k],
+            to // groups, lax.rem(to, groups),
+        )
+
+    def block_in(k):
+        at = lax.rem(me + groups - k, groups)
+        return remote(pooled_ref.at[at], large_out.at[at], send.at[k], recv.at[k], rep, at)
+
+    def ids_in(k):
+        at = lax.rem(index + devices - k, devices)
+        return remote(
+            ids_ref.at[at], ids_out.at[at], id_send.at[k], id_recv.at[k],
+            at // groups, lax.rem(at, groups),
+        )
+
+    def run(low, high, act):
+        def body(k, c):
+            act(k)
+            return c
+
+        lax.fori_loop(low, high, body, 0)
+
+    greet_all()
+    run(1, groups, lambda k: block(k).start())
+    run(1, devices, lambda k: ids(k).start())
+    mine = pltpu.make_async_copy(pooled_ref.at[me], large_out.at[me], own.at[0])
+    mine_ids = pltpu.make_async_copy(ids_ref.at[index], ids_out.at[index], own.at[1])
+    mine.start()
+    mine_ids.start()
+    mine.wait()
+    mine_ids.wait()
+    run(1, groups, lambda k: block_in(k).wait_recv())
+    run(1, devices, lambda k: ids_in(k).wait_recv())
+    run(1, groups, lambda k: block(k).wait_send())
+    run(1, devices, lambda k: ids(k).wait_send())
+
+
+def forward(pooled, ids):
+    groups, devices = pooled.shape[0], ids.shape[0]
+    return pl.pallas_call(
+        forward_kernel,
+        out_shape=(
+            jax.ShapeDtypeStruct(pooled.shape, pooled.dtype),
+            jax.ShapeDtypeStruct(ids.shape, ids.dtype),
+        ),
+        in_specs=[whole(pltpu.VMEM)] * 2,
+        out_specs=(whole(pltpu.VMEM), whole(pltpu.VMEM)),
+        scratch_shapes=[pltpu.SemaphoreType.DMA((groups,))] * 2
+        + [pltpu.SemaphoreType.DMA((devices,))] * 2
+        + [pltpu.SemaphoreType.DMA((2,))],
+        compiler_params=pltpu.CompilerParams(
+            collective_id=0, has_side_effects=True, vmem_limit_bytes=VMEM_LIMIT
+        ),
+        name="forward",
+    )(pooled, ids)
+
+
+def fold_kernel(fold_ref, out_ref, send, recv, far_send, far_recv, own):
+    copies, groups = lax.axis_size("rep"), lax.axis_size("shard")
+    rep, me = lax.axis_index("rep"), lax.axis_index("shard")
+    other = 1 - rep
+
+    def out_block(k):
+        to = lax.rem(me + k, groups)
+        return remote(
+            fold_ref.at[to], out_ref.at[rep * groups + me], send.at[k], recv.at[k], rep, to
+        )
+
+    def in_block(k):
+        at = lax.rem(me + groups - k, groups)
+        return remote(
+            fold_ref.at[at], out_ref.at[rep * groups + at], send.at[k], recv.at[k], rep, at
+        )
+
+    def far_out(k):
+        slot = out_ref.at[rep * groups + lax.rem(me + groups - k, groups)]
+        return remote(slot, slot, far_send.at[k], far_recv.at[k], other, me)
+
+    def far_in(k):
+        slot = out_ref.at[other * groups + lax.rem(me + groups - k, groups)]
+        return remote(slot, slot, far_send.at[k], far_recv.at[k], other, me)
+
+    own_far = remote(
+        fold_ref.at[me], out_ref.at[rep * groups + me], far_send.at[0], far_recv.at[0], other, me
+    )
+
+    def run(act):
+        def body(k, c):
+            act(k)
+            return c
+
+        lax.fori_loop(1, groups, body, 0)
+
+    greet_all()
+    run(lambda k: out_block(k).start())
+    own_far.start()
+    mine = pltpu.make_async_copy(fold_ref.at[me], out_ref.at[rep * groups + me], own.at[0])
+    mine.start()
+
+    def pass_on(k):
+        in_block(k).wait_recv()
+        far_out(k).start()
+
+    run(pass_on)
+    mine.wait()
+    far_in(0).wait_recv()
+    run(lambda k: far_in(k).wait_recv())
+    own_far.wait_send()
+    run(lambda k: far_out(k).wait_send())
+    run(lambda k: out_block(k).wait_send())
+
+
+def fold_exchange(fold, copies):
+    groups = fold.shape[0]
+    return pl.pallas_call(
+        fold_kernel,
+        out_shape=jax.ShapeDtypeStruct((copies * groups,) + fold.shape[1:], fold.dtype),
+        in_specs=[whole(pltpu.VMEM)],
+        out_specs=whole(pltpu.VMEM),
+        scratch_shapes=[pltpu.SemaphoreType.DMA((groups,))] * 4 + [pltpu.SemaphoreType.DMA((1,))],
+        compiler_params=pltpu.CompilerParams(
+            collective_id=1, has_side_effects=True, vmem_limit_bytes=VMEM_LIMIT
+        ),
+        name="fold_exchange",
+    )(fold)
+
+
+def spread_kernel(own_ref, out_ref, send_z, send_1, send_2, send_core, recv, local):
+    groups = lax.axis_size("shard")
+    ring = groups // 4
+    rep, member = lax.axis_index("rep"), lax.axis_index("shard")
+    z, y, core = member // 4, lax.rem(member, 4) // 2, lax.rem(member, 2)
+
+    def shard_of(z_at, y_at, core_at):
+        return z_at * 4 + y_at * 2 + core_at
+
+    def send(h, src, rep_at, z_at, y_at, sem, to_rep, to_z, to_y, to_core):
+        slot = rep_at * groups + shard_of(z_at, y_at, core)
+        source = out_ref.at[slot, h] if src is None else src
+        return remote(
+            source, out_ref.at[slot, h], sem, recv.at[h, slot],
+            to_rep, shard_of(to_z, to_y, to_core),
+        )
+
+    def arrived(h, rep_at, z_at, y_at, core_at):
+        slot = rep_at * groups + shard_of(z_at, y_at, core_at)
+        place = out_ref.at[slot, h]
+        remote(place, place, local.at[1], recv.at[h, slot], rep, member).wait_recv()
+
+    greet_all()
+    pending = []
+
+    def go(copy):
+        copy.start()
+        pending.append(copy)
+
+    def second(h, k, src, rep_at, z_at, y_at):
+        hop = (rep, z, 1 - y, core) if h == 0 else (1 - rep, z, y, core)
+        go(send(h, src, rep_at, z_at, y_at, send_1.at[h, k], *hop))
+
+    def third(h, k, src, rep_at, z_at, y_at):
+        hop = (1 - rep, z, y, core) if h == 0 else (rep, z, 1 - y, core)
+        go(send(h, src, rep_at, z_at, y_at, send_2.at[h, k], *hop))
+
+    def last(h, k, src, rep_at, z_at, y_at):
+        go(send(h, src, rep_at, z_at, y_at, send_core.at[h, k], rep, z, y, 1 - core))
+
+    for k in range(1, ring):
+        for h in range(2):
+            go(send(h, own_ref.at[h], rep, z, y, send_z.at[h, k], rep, lax.rem(z + k, ring), y, core))
+    for h in range(2):
+        src = own_ref.at[h]
+        second(h, 0, src, rep, z, y)
+        third(h, 0, src, rep, z, y)
+        last(h, 0, src, rep, z, y)
+    mine = pltpu.make_async_copy(
+        own_ref, out_ref.at[rep * groups + member], local.at[0]
+    )
+    mine.start()
+    for k in range(1, ring):
+        z_at = lax.rem(z + ring - k, ring)
+        for h in range(2):
+            arrived(h, rep, z_at, y, core)
+            second(h, k, None, rep, z_at, y)
+            third(h, k, None, rep, z_at, y)
+            last(h, k, None, rep, z_at, y)
+    for k in range(ring):
+        z_at = lax.rem(z + ring - k, ring)
+        for h in range(2):
+            where = (rep, z_at, 1 - y) if h == 0 else (1 - rep, z_at, y)
+            arrived(h, *where, core)
+            third(h, ring + k, None, *where)
+            last(h, ring + k, None, *where)
+    for k in range(2 * ring):
+        z_at = lax.rem(z + ring - k % ring, ring)
+        for h in range(2):
+            if h == 0:
+                where = (1 - rep, z_at, y if k < ring else 1 - y)
+            else:
+                where = (rep if k < ring else 1 - rep, z_at, 1 - y)
+            arrived(h, *where, core)
+            last(h, 2 * ring + k, None, *where)
+    for r in range(2):
+        for k in range(ring):
+            for y_at in range(2):
+                for h in range(2):
+                    arrived(h, r, k, y_at, 1 - core)
+    mine.wait()
+    for copy in pending:
+        copy.wait_send()
+
+
+def spread_all(own, copies, groups):
+    rows, width = own.shape
+    ring = groups // 4
+    devices = copies * groups
+    out = pl.pallas_call(
+        spread_kernel,
+        out_shape=jax.ShapeDtypeStruct((devices, 2, rows // 2, width), own.dtype),
+        in_specs=[whole(pltpu.VMEM)],
+        out_specs=whole(pltpu.VMEM),
+        scratch_shapes=[
+            pltpu.SemaphoreType.DMA((2, ring)),
+            pltpu.SemaphoreType.DMA((2, ring)),
+            pltpu.SemaphoreType.DMA((2, 2 * ring)),
+            pltpu.SemaphoreType.DMA((2, 4 * ring)),
+            pltpu.SemaphoreType.DMA((2, devices)),
+            pltpu.SemaphoreType.DMA((2,)),
+        ],
+        compiler_params=pltpu.CompilerParams(
+            collective_id=2, has_side_effects=True, vmem_limit_bytes=VMEM_LIMIT
+        ),
+        name="spread_all",
+    )(own.reshape(2, rows // 2, width))
+    return out.reshape(devices * rows, width)
 
 
 def shards(
@@ -311,44 +598,31 @@
 ):
     groups = lax.axis_size("shard")
     copies = lax.axis_size("rep")
-    replica = lax.axis_index("rep")
-    member = lax.axis_index("shard")
     devices = groups * copies
-    index = replica * groups + member
+    first = lax.axis_index("rep") * groups
+    index = first + lax.axis_index("shard")
     small_count, small_rows, width = small_tables.shape
-    batch = dense.shape[0]
     per_table = devices // small_count
-
-    ids_by_table = jnp.transpose(small_ids)
-    sent_ids = jnp.repeat(ids_by_table, per_table, axis=0)
-    all_ids = lax.all_to_all(sent_ids, ("rep", "shard"), split_axis=0, concat_axis=0, tiled=True)
-
     ends, rows, table = bag_ends[0], owner_row_index[0], large_tables[0]
-    counts = ends[:, -1]
-    first = replica * groups
-
-    def mine(x):
-        return lax.dynamic_slice_in_dim(x, first, groups, 0)
-
-    pooled = pool(mine(rows), mine(counts), mine(ends), table)
-    large = lax.all_to_all(pooled, "shard", split_axis=0, concat_axis=0, tiled=True)
-    sizes = lax.dynamic_slice_in_dim(batch_sizes, index, 1, 1)[:, 0]
+
+    sent_ids = jnp.repeat(jnp.transpose(small_ids), per_table, axis=0)[:, None]
+    pooled = pool(first[None], groups, rows, ends, table)
+    large, all_ids = forward(pooled, sent_ids)
     small_grads, fold = top(
-        sizes, dense, small_ids, labels, small_tables, large, w_first, b_first, w_out
+        index[None], batch_sizes, dense, small_ids, labels, small_tables, large, w_first,
+        b_first, w_out,
     )
-    fold_back = lax.all_to_all(fold, "shard", split_axis=0, concat_axis=0, tiled=True)
-    fold_all = lax.all_gather(fold_back, "rep", axis=0, tiled=True)
+    fold_all = fold_exchange(fold, copies)
     sent = jnp.repeat(small_grads, per_table, axis=0)
+    sent, fold_all = lax.optimization_barrier((sent, fold_all))
     arrived = lax.all_to_all(sent, ("rep", "shard"), split_axis=0, concat_axis=0, tiled=True)
+    large_new = scatter(rows, ends, fold_all, table)
     part_rows = small_count * small_rows // devices
     flat = small_tables.reshape(small_count * small_rows, width)
     own = lax.dynamic_slice_in_dim(flat, index * part_rows, part_rows, 0)
     first_row = (lax.rem(index, per_table) * part_rows)[None].astype(jnp.int32)
-    updated = small_update(first_row, all_ids, arrived, own)
-    small_new = lax.all_gather(updated, ("rep", "shard"), axis=0, tiled=True).reshape(
-        small_count, small_rows, width
-    )
-    large_new = scatter(rows, counts, ends, fold_all, table)
+    updated = small_update(first_row, all_ids[:, 0], arrived, own)
+    small_new = spread_all(updated, copies, groups).reshape(small_count, small_rows, width)
     return small_new, large_new[None]
 
 

time: 243 us -> 200 us (0.82)
  Pallas kernels: 78.8 us -> 161 us
  waiting for transfers between devices: 94.2 us -> 19.6 us
  blocking collectives: 20.3 us -> 0 us
  between operations: 14.1 us -> 0.68 us
  starting transfers between devices: 16.8 us -> 6.31 us
  local copies, waits for them, and re-layouts: 17.6 us -> 12.5 us
    pallas_call x0 -> x3, Pallas kernels: none -> 78.3 us  [the longest x1 30.4 us: spread_all(): pl.pallas_call(spread_kernel, out_shape=jax.ShapeDtypeStruct((devices, 2,...]
    all_gather x2 -> x0, waiting for transfers between devices: 32.7 us -> none  [the longest x1 32.7 us: shards(): lax.all_gather(updated, ('rep', 'shard'), axis=0, tiled=True)]
    all_to_all x1, waiting for transfers between devices: 47.2 us -> 19.6 us  [shards(): lax.all_to_all(sent, ('rep', 'shard'), split_axis=0, concat_axis=0, tiled...]
    all_to_all x1 -> x0, blocking collectives: 20.3 us -> none  [shards(): lax.all_to_all(fold, 'shard', split_axis=0, concat_axis=0, tiled=True)]
    all_to_all x2 -> x0, waiting for transfers between devices: 13.6 us -> none  [the longest x1 13.6 us: shards(): lax.all_to_all(pooled, 'shard', split_axis=0, concat_axis=0, tiled=True)]
    all_to_all x2 -> x0, starting transfers between devices: 12.6 us -> none  [the longest x1 9.49 us: shards(): lax.all_to_all(pooled, 'shard', split_axis=0, concat_axis=0, tiled=True)]
    dynamic_slice x4 -> x0, local copies, waits for them, and re-layouts: 4.08 us -> none  [the longest x3 3.31 us: mine(): return lax.dynamic_slice_in_dim(x, first, groups, 0)]
    slice x2 -> x0, local copies, waits for them, and re-layouts: 3.15 us -> none  [the longest x1 1.66 us: top(): w_first[pair_count:]]
  transfers between devices with their start and end apart: 5 -> 1, of which waited for: 3 -> 1; matrix products, arithmetic and copies ran while one was open for 3% -> 1% of each run, Pallas kernels for 27% -> 14%
where the time goes in v2:
time: 200 us
  Pallas kernels  161 us (80%)
  waiting for transfers between devices  19.6 us (10%)
  local copies, waits for them, and re-layouts  12.5 us (6%)
  starting transfers between devices  6.31 us (3%)
    pallas_call x1, Pallas kernels, spread_all(): pl.pallas_call(spread_kernel, out_shape=jax.ShapeDtypeStruct((devices, 2,...  30.4 us
    pallas_call x1, Pallas kernels, top(): pl.pallas_call(functools.partial(top_kernel, vec_count, pad), out_shape=(...  28.8 us
    pallas_call x1, Pallas kernels, scatter(): pl.pallas_call(scatter_kernel, out_shape=jax.ShapeDtypeStruct(table.shape...  28.1 us
    pallas_call x1, Pallas kernels, fold_exchange(): pl.pallas_call(fold_kernel, out_shape=jax.ShapeDtypeStruct((copies * grou...  24 us
    pallas_call x1, Pallas kernels, forward(): pl.pallas_call(forward_kernel, out_shape=(jax.ShapeDtypeStruct(pooled.sha...  23.9 us
    all_to_all x1, waiting for transfers between devices, shards(): lax.all_to_all(sent, ('rep', 'shard'), split_axis=0, concat_axis=0, tiled...  19.6 us
    pallas_call x1, Pallas kernels, pool(): pl.pallas_call(pool_kernel, out_shape=jax.ShapeDtypeStruct((owners, ends....  15.3 us
    pallas_call x1, Pallas kernels, small_update(): pl.pallas_call(functools.partial(small_kernel, rows.shape[0]), out_shape=...  10.2 us
  transfers between devices with their start and end apart: 1, of which 1 were waited for; matrix products, arithmetic and copies ran while one was open for 1% of the time, Pallas kernels for 14%

profile of v2, /device:TPU:0, one launch (start us, length us, event | category | flops | bytes accessed | tf_op | source)
XLA Modules:
  0.0 199.7 jit_solution(3817104336178022729)
XLA Ops:
  0.6 1.5 copy.14.ids_ref
  2.1 1.4 broadcast_in_dim.23.ids_ref
  3.5 1.5 copy.15.labels_ref
  5.0 15.3 %pool.1.pooled_ref = bf16[16,128,128]{2,1,0:T(8,128)(2,1)} custom-call(s32[1]{0:T(128)} %bitcast.first_ref, s32[32,256]{1,0:T(8,128)} %bitcast.27, s32[32,128]{1,0:T(8,128)} %bitcast.23, s32[32,128]{1,0:T(8,128)} %bitcast.24, bf16[8192,128]{1,0:T(8,128)(2,1)} %bitcast.18), custom_call_target="tpu_custom_call" | custom-call | tf_op jit(solution)/shard_map/pool/pallas_call | solution.py:64
  20.3 23.9 %forward.1 = (bf16[16,128,128]{2,1,0:T(8,128)(2,1)}, s32[32,1,256]{2,1,0:T(1,128)}) custom-call(bf16[16,128,128]{2,1,0:T(8,128)(2,1)} %pool.1.pooled_ref, s32[32,1,256]{2,1,0:T(1,128)} %broadcast_in_dim.23.ids_ref), custom_call_target="tpu_custom_call" | custom-call | tf_op jit(solution)/shard_map/forward/pallas_call | solution.py:397
  44.2 28.8 %top.1 = (bf16[32,256,128]{2,1,0:T(8,128)(2,1)}, bf16[16,128,128]{2,1,0:T(8,128)(2,1)}) custom-call(s32[1]{0:T(128)} %bitcast.5.index_ref, s32[16,32]{1,0:T(8,128)} %sizes_ref.1, bf16[256,128]{1,0:T(8,128)(2,1)} %dense_ref.1, s32[256,32]{1,0:T(8,128)} %copy.14.ids_ref, s32[256,1]{1,0:T(8,128)} %copy.15.labels_ref, bf16[32,512,128]{2,1,0:T(8,128)(2,1)} %tables_ref.1, ...), custom_call_target="tpu_custom_call" | custom-call | tf_op jit(solution)/shard_map/top/pallas_call | solution.py:296
  73.0 0.0 copy-start.1
  73.0 24.0 %fold_exchange.1.fold_ref = bf16[32,128,128]{2,1,0:T(8,128)(2,1)} custom-call(bf16[16,128,128]{2,1,0:T(8,128)(2,1)} %get-tuple-element.11.fold_ref), custom_call_target="tpu_custom_call" | custom-call | tf_op jit(solution)/shard_map/fold_exchange/pallas_call | solution.py:472
  97.0 6.3 %all-to-all-start = ((bf16[32,256,128]{2,1,0:T(8,128)(2,1)}), bf16[32,256,128]{2,1,0:T(8,128)(2,1)S(1)}, u32[]{:S(2)}, u32[]{:S(2)}) async-start(bf16[32,256,128]{2,1,0:T(8,128)(2,1)} %get-tuple-element.12), calls=%async_computation | async-start | bytes 4194304 | tf_op jit(solution)/shard_map/all_to_all | solution.py:618
  103.3 0.0 copy-done.1
  103.3 0.6 copy.18
  103.9 1.6 constant_dynamic-slice_fusion.table_ref
  105.5 28.1 %scatter.1 = bf16[8192,128]{1,0:T(8,128)(2,1)} custom-call(s32[32,256]{1,0:T(8,128)} %bitcast.28, s32[32,128]{1,0:T(8,128)} %bitcast.25, s32[32,128]{1,0:T(8,128)} %bitcast.26, bf16[32,128,128]{2,1,0:T(8,128)(2,1)} %fold_exchange.1.fold_ref, bf16[8192,128]{1,0:T(8,128)(2,1)} %bitcast.19), custom_call_target="tpu_custom_call" | custom-call | flops 2684354560 | bytes 4194304 | tf_op jit(solution)/shard_map/scatter/pallas_call | solution.py:121
  133.6 19.6 %all-to-all-done.grads_ref = bf16[32,256,128]{2,1,0:T(8,128)(2,1)S(1)} async-done(((bf16[32,256,128]{2,1,0:T(8,128)(2,1)}), bf16[32,256,128]{2,1,0:T(8,128)(2,1)S(1)}, u32[]{:S(2)}, u32[]{:S(2)}) %all-to-all-start) | async-done | bytes 2097184 | tf_op jit(solution)/shard_map/all_to_all | solution.py:618
  153.2 0.0 copy-start
  153.2 1.3 copy-done
  154.5 10.2 %small_update.1 = bf16[512,128]{1,0:T(8,128)(2,1)} custom-call(s32[1]{0:T(128)} %constant.7.clone.1.first_ref, s32[32,256]{1,0:T(8,128)} %bitcast.22, bf16[32,256,128]{2,1,0:T(8,128)(2,1)} %copy-done, bf16[512,128]{1,0:T(8,128)(2,1)} %constant_dynamic-slice_fusion.table_ref), custom_call_target="tpu_custom_call" | custom-call | tf_op jit(solution)/shard_map/small_update/pallas_call | solution.py:150
  164.7 30.4 %spread_all.1 = bf16[32,2,256,128]{3,2,1,0:T(8,128)(2,1)} custom-call(bf16[2,256,128]{2,1,0:T(8,128)(2,1)} %bitcast.20), custom_call_target="tpu_custom_call" | custom-call | tf_op jit(solution)/shard_map/spread_all/pallas_call | solution.py:574
  195.1 4.7 %copy.20 = bf16[32,512,128]{2,1,0:T(8,128)(2,1)} copy(bf16[32,512,128]{2,1,0:T(8,128)(2,1)} %bitcast.16) | data formatting | bytes 8388608
Async XLA Ops:
  73.0 30.3 %copy-start.1 = (s32[32,1,256]{2,1,0:T(1,128)S(1)}, s32[32,1,256]{2,1,0:T(1,128)}, u32[]{:S(2)}) copy-start(s32[32,1,256]{2,1,0:T(1,128)} %get-tuple-element.8) | copy-start | bytes 98308
  97.0 56.2 %all-to-all-start = ((bf16[32,256,128]{2,1,0:T(8,128)(2,1)}), bf16[32,256,128]{2,1,0:T(8,128)(2,1)S(1)}, u32[]{:S(2)}, u32[]{:S(2)}) async-start(bf16[32,256,128]{2,1,0:T(8,128)(2,1)} %get-tuple-element.12), calls=%async_computation | async-start | bytes 4194304 | tf_op jit(solution)/shard_map/all_to_all | solution.py:618
  153.2 1.3 copy-start

commit v3 on v2

--- a/solution.py
+++ b/solution.py
@@ -43,19 +43,23 @@
         def group(g, c):
             base = pl.multiple_of(g * 8, 8)
             parts = [wide[pl.ds(rows_ref[d, base + u], 1), :] for u in range(8)]
-            picked[pl.ds(base, 8), :] = jnp.concatenate(parts, axis=0)
+            picked[pl.ds(pl.multiple_of(o * slots + base, 8), 8), :] = jnp.concatenate(parts, axis=0)
             return c
 
-        lax.fori_loop(0, (count_ref[d, last] + 7) // 8, group, 0)
-        members = members_of(ends_ref[pl.ds(d, 1), :], slots)
+        return lax.fori_loop(0, (count_ref[d, last] + 7) // 8, group, carry)
+
+    lax.fori_loop(0, owners, owner, 0)
+
+    def sums(o, carry):
+        members = members_of(ends_ref[pl.ds(o + first, 1), :], slots)
+        block = picked[pl.ds(pl.multiple_of(o * slots, 8), slots), :].astype(bf16)
         pooled = lax.dot_general(
-            members, picked[...].astype(bf16), (((0,), (0,)), ((), ())),
-            preferred_element_type=f32,
+            members, block, (((0,), (0,)), ((), ())), preferred_element_type=f32
         )
         out_ref[o] = pooled.astype(bf16)
         return carry
 
-    lax.fori_loop(0, owners, owner, 0)
+    lax.fori_loop(0, owners, sums, 0, unroll=4)
 
 
 def pool(first, owners, rows, ends, table):
@@ -68,7 +72,7 @@
         out_specs=whole(pltpu.VMEM),
         scratch_shapes=[
             pltpu.VMEM(table.shape, f32),
-            pltpu.VMEM((slots, width), f32),
+            pltpu.VMEM((owners * slots, width), f32),
         ],
         compiler_params=pltpu.CompilerParams(vmem_limit_bytes=VMEM_LIMIT),
         name="pool",
@@ -82,13 +86,19 @@
     for total in sums:
         total[...] = jnp.zeros_like(total)
 
+    def expand(d, carry):
+        members = members_of(ends_ref[pl.ds(d, 1), :], slots)
+        spread[pl.ds(pl.multiple_of(d * slots, 8), slots), :] = jnp.dot(
+            members, fold_ref[d], preferred_element_type=f32
+        )
+        return carry
+
+    lax.fori_loop(0, owners, expand, 0, unroll=4)
+
     def owner(d, carry):
-        members = members_of(ends_ref[pl.ds(d, 1), :], slots)
-        spread[...] = jnp.dot(members, fold_ref[d], preferred_element_type=f32)
-
         def group(g, c):
             base = pl.multiple_of(g * 8, 8)
-            block = spread[pl.ds(base, 8), :]
+            block = spread[pl.ds(pl.multiple_of(d * slots + base, 8), 8), :]
             for u in range(0, 8, lanes_of):
                 spots = [rows_ref[d, base + u + v] for v in range(lanes_of)]
                 news = [
@@ -99,8 +109,7 @@
                     sums[v][pl.ds(spots[v], 1), :] = news[v]
             return c
 
-        lax.fori_loop(0, (count_ref[d, last] + 7) // 8, group, 0)
-        return carry
+        return lax.fori_loop(0, (count_ref[d, last] + 7) // 8, group, carry)
 
     lax.fori_loop(0, owners, owner, 0)
     step = 256
@@ -123,7 +132,7 @@
         out_shape=jax.ShapeDtypeStruct(table.shape, bf16),
         in_specs=[whole(pltpu.SMEM), whole(pltpu.SMEM)] + [whole(pltpu.VMEM)] * 3,
         out_specs=whole(pltpu.VMEM),
-        scratch_shapes=[pltpu.VMEM((slots, table.shape[1]), f32)]
+        scratch_shapes=[pltpu.VMEM((rows.size, table.shape[1]), f32)]
         + [pltpu.VMEM(table.shape, f32)] * 4,
         compiler_params=pltpu.CompilerParams(vmem_limit_bytes=VMEM_LIMIT),
         cost_estimate=pl.CostEstimate(
@@ -142,7 +151,7 @@
         hot = (rows == ids_ref[pl.ds(s, 1), :]).astype(f32).astype(bf16)
         return total + jnp.dot(hot, grads_ref[s], preferred_element_type=f32)
 
-    total = lax.fori_loop(0, senders, one, total)
+    total = lax.fori_loop(0, senders, one, total, unroll=8)
     out_ref[...] = (table_ref[...].astype(f32) - step_size * total).astype(bf16)
 
 
@@ -162,11 +171,11 @@
 
 
 def top_kernel(
-    vec_count, pad, index_ref, sizes_ref, dense_ref, ids_ref, labels_ref, tables_ref, large_ref,
+    vec_count, pad, index_ref, sizes_ref, dense_ref, labels_ref, small_ref, large_ref,
     w_ref, bias_ref, wout_ref, small_out, fold_out, vecs, gram, pairs, spread,
 ):
     batch, width = dense_ref.shape
-    small_count, small_rows = tables_ref.shape[0], tables_ref.shape[1]
+    small_count = small_ref.shape[0]
     feats, bag_span = large_ref.shape[0], large_ref.shape[1]
     pair_pad = pairs.shape[1]
     pair_count = vec_count * (vec_count - 1) // 2
@@ -177,10 +186,8 @@
         return pl.ds(i, batch, stride=pad)
 
     vecs[rows_of(0), :] = dense_ref[...].astype(f32)
-    rows = iota((batch, small_rows), 1)
     for t in range(small_count):
-        hot = (ids_ref[:, t : t + 1] == rows).astype(f32).astype(bf16)
-        vecs[rows_of(1 + t), :] = jnp.dot(hot, tables_ref[t], preferred_element_type=f32)
+        vecs[rows_of(1 + t), :] = small_ref[t].astype(f32)
     sample = iota((batch, bag_span), 0)
     bag = iota((batch, bag_span), 1) * batch
     for f in range(feats):
@@ -286,9 +293,9 @@
         ).astype(bf16)
 
 
-def top(index, sizes, dense, ids, labels, tables, large, w_first, bias, wout):
+def top(index, sizes, dense, labels, small, large, w_first, bias, wout):
     batch, width = dense.shape
-    small_count, feats, bag_span = tables.shape[0], large.shape[0], large.shape[1]
+    small_count, feats, bag_span = small.shape[0], large.shape[0], large.shape[1]
     vec_count = 1 + small_count + feats
     pad = -(-vec_count // 8) * 8
     pair_count = vec_count * (vec_count - 1) // 2
@@ -299,7 +306,7 @@
             jax.ShapeDtypeStruct((small_count, batch, width), bf16),
             jax.ShapeDtypeStruct((feats, bag_span, width), bf16),
         ),
-        in_specs=[whole(pltpu.SMEM)] * 2 + [whole(pltpu.VMEM)] * 8,
+        in_specs=[whole(pltpu.SMEM)] * 2 + [whole(pltpu.VMEM)] * 7,
         out_specs=(whole(pltpu.VMEM), whole(pltpu.VMEM)),
         scratch_shapes=[
             pltpu.VMEM((batch * pad, width), f32),
@@ -310,7 +317,7 @@
         compiler_params=pltpu.CompilerParams(vmem_limit_bytes=VMEM_LIMIT),
         name="top",
     )(
-        index, sizes, dense, ids, labels[:, None], tables, large, w_first,
+        index, sizes, dense, labels[:, None], small, large, w_first,
         bias[None, :], wout[None, :],
     )
 
@@ -341,7 +348,8 @@
 
 
 def forward_kernel(
-    pooled_ref, ids_ref, large_out, ids_out, send, recv, id_send, id_recv, own
+    pooled_ref, ids_ref, own_ids_ref, tables_ref, large_out, ids_out, small_out,
+    send, recv, id_send, id_recv, own,
 ):
     copies, groups = lax.axis_size("rep"), lax.axis_size("shard")
     devices = copies * groups
@@ -384,6 +392,11 @@
     mine_ids = pltpu.make_async_copy(ids_ref.at[index], ids_out.at[index], own.at[1])
     mine.start()
     mine_ids.start()
+    batch, small_count = own_ids_ref.shape
+    rows = iota((batch, tables_ref.shape[1]), 1)
+    for t in range(small_count):
+        hot = (own_ids_ref[:, t : t + 1] == rows).astype(f32).astype(bf16)
+        small_out[t] = jnp.dot(hot, tables_ref[t], preferred_element_type=f32).astype(bf16)
     mine.wait()
     mine_ids.wait()
     run(1, groups, lambda k: block_in(k).wait_recv())
@@ -392,16 +405,19 @@
     run(1, devices, lambda k: ids(k).wait_send())
 
 
-def forward(pooled, ids):
+def forward(pooled, ids, own_ids, tables):
     groups, devices = pooled.shape[0], ids.shape[0]
     return pl.pallas_call(
         forward_kernel,
         out_shape=(
             jax.ShapeDtypeStruct(pooled.shape, pooled.dtype),
             jax.ShapeDtypeStruct(ids.shape, ids.dtype),
+            jax.ShapeDtypeStruct(
+                (tables.shape[0], own_ids.shape[0], tables.shape[2]), tables.dtype
+            ),
         ),
-        in_specs=[whole(pltpu.VMEM)] * 2,
-        out_specs=(whole(pltpu.VMEM), whole(pltpu.VMEM)),
+        in_specs=[whole(pltpu.VMEM)] * 4,
+        out_specs=(whole(pltpu.VMEM),) * 3,
         scratch_shapes=[pltpu.SemaphoreType.DMA((groups,))] * 2
         + [pltpu.SemaphoreType.DMA((devices,))] * 2
         + [pltpu.SemaphoreType.DMA((2,))],
@@ -409,7 +425,7 @@
             collective_id=0, has_side_effects=True, vmem_limit_bytes=VMEM_LIMIT
         ),
         name="forward",
-    )(pooled, ids)
+    )(pooled, ids, own_ids, tables)
 
 
 def fold_kernel(fold_ref, out_ref, send, recv, far_send, far_recv, own):
@@ -477,6 +493,9 @@
         scratch_shapes=[pltpu.SemaphoreType.DMA((groups,))] * 4 + [pltpu.SemaphoreType.DMA((1,))],
         compiler_params=pltpu.CompilerParams(
             collective_id=1, has_side_effects=True, vmem_limit_bytes=VMEM_LIMIT
+        ),
+        cost_estimate=pl.CostEstimate(
+            flops=400 * fold.size * LANES, bytes_accessed=4 * fold.size, transcendentals=0
         ),
         name="fold_exchange",
     )(fold)
@@ -607,14 +626,12 @@
 
     sent_ids = jnp.repeat(jnp.transpose(small_ids), per_table, axis=0)[:, None]
     pooled = pool(first[None], groups, rows, ends, table)
-    large, all_ids = forward(pooled, sent_ids)
+    large, all_ids, small = forward(pooled, sent_ids, small_ids, small_tables)
     small_grads, fold = top(
-        index[None], batch_sizes, dense, small_ids, labels, small_tables, large, w_first,
-        b_first, w_out,
+        index[None], batch_sizes, dense, labels, small, large, w_first, b_first, w_out
     )
     fold_all = fold_exchange(fold, copies)
     sent = jnp.repeat(small_grads, per_table, axis=0)
-    sent, fold_all = lax.optimization_barrier((sent, fold_all))
     arrived = lax.all_to_all(sent, ("rep", "shard"), split_axis=0, concat_axis=0, tiled=True)
     large_new = scatter(rows, ends, fold_all, table)
     part_rows = small_count * small_rows // devices

time: 200 us -> 211 us (1.055)
  Pallas kernels: 161 us -> 193 us
  waiting for transfers between devices: 19.6 us -> 0.01 us
  starting transfers between devices: 6.31 us -> 3.8 us
    pallas_call x1, Pallas kernels: 24 us -> 65.4 us  [fold_exchange(): pl.pallas_call(fold_kernel, out_shape=jax.ShapeDtypeStruct((copies * grou...]
    all_to_all x1, waiting for transfers between devices: 19.6 us -> 0.01 us  [shards(): lax.all_to_all(sent, ('rep', 'shard'), split_axis=0, concat_axis=0, tiled...]
    pallas_call x1, Pallas kernels: 28.1 us -> 21.5 us  [scatter(): pl.pallas_call(scatter_kernel, out_shape=jax.ShapeDtypeStruct(table.shape...]
    pallas_call x1, Pallas kernels: 10.2 us -> 5.15 us  [small_update(): pl.pallas_call(functools.partial(small_kernel, rows.shape[0]), out_shape=...]
    pallas_call x1, Pallas kernels: 30.4 us -> 34.9 us  [spread_all(): pl.pallas_call(spread_kernel, out_shape=jax.ShapeDtypeStruct((devices, 2,...]
    pallas_call x1, Pallas kernels: 23.9 us -> 27.6 us  [forward(): pl.pallas_call(forward_kernel, out_shape=(jax.ShapeDtypeStruct(pooled.sha...]
    pallas_call x1, Pallas kernels: 15.3 us -> 12 us  [pool(): pl.pallas_call(pool_kernel, out_shape=jax.ShapeDtypeStruct((owners, ends....]
    all_to_all x1, starting transfers between devices: 6.31 us -> 3.8 us  [shards(): lax.all_to_all(sent, ('rep', 'shard'), split_axis=0, concat_axis=0, tiled...]
  transfers between devices with their start and end apart: 1 -> 1, of which waited for: 1 -> 0; matrix products, arithmetic and copies ran while one was open for 1% -> 1% of each run, Pallas kernels for 14% -> 41%
where the time goes in v3:
time: 211 us; the launch traced here: 210 us
  Pallas kernels  193 us (91%)
  local copies, waits for them, and re-layouts  12.5 us (6%)
  starting transfers between devices  3.8 us (2%)
    pallas_call x1, Pallas kernels, fold_exchange(): pl.pallas_call(fold_kernel, out_shape=jax.ShapeDtypeStruct((copies * grou...  65.4 us
    pallas_call x1, Pallas kernels, spread_all(): pl.pallas_call(spread_kernel, out_shape=jax.ShapeDtypeStruct((devices, 2,...  34.9 us
    pallas_call x1, Pallas kernels, forward(): pl.pallas_call(forward_kernel, out_shape=(jax.ShapeDtypeStruct(pooled.sha...  27.6 us
    pallas_call x1, Pallas kernels, top(): pl.pallas_call(functools.partial(top_kernel, vec_count, pad), out_shape=(...  26.9 us
    pallas_call x1, Pallas kernels, scatter(): pl.pallas_call(scatter_kernel, out_shape=jax.ShapeDtypeStruct(table.shape...  21.5 us
    pallas_call x1, Pallas kernels, pool(): pl.pallas_call(pool_kernel, out_shape=jax.ShapeDtypeStruct((owners, ends....  12 us
    unnamed x7, local copies, waits for them, and re-layouts  8.1 us
    pallas_call x1, Pallas kernels, small_update(): pl.pallas_call(functools.partial(small_kernel, rows.shape[0]), out_shape=...  5.15 us
  transfers between devices with their start and end apart: 1, of which 0 were waited for; matrix products, arithmetic and copies ran while one was open for 1% of the time, Pallas kernels for 41%

profile of v3, /device:TPU:0, one launch (start us, length us, event | category | flops | bytes accessed | tf_op | source)
XLA Modules:
  0.0 210.5 jit_solution(9491552439388971187)
XLA Ops:
  0.6 1.5 copy.14.own_ids_ref
  2.1 1.4 broadcast_in_dim.23.ids_ref
  3.5 1.5 copy.15.labels_ref
  5.0 12.0 %pool.1.pooled_ref = bf16[16,128,128]{2,1,0:T(8,128)(2,1)} custom-call(s32[1]{0:T(128)} %bitcast.first_ref, s32[32,256]{1,0:T(8,128)} %bitcast.27, s32[32,128]{1,0:T(8,128)} %bitcast.23, s32[32,128]{1,0:T(8,128)} %bitcast.24, bf16[8192,128]{1,0:T(8,128)(2,1)} %bitcast.18), custom_call_target="tpu_custom_call" | custom-call | tf_op jit(solution)/shard_map/pool/pallas_call | solution.py:68
  17.0 27.6 %forward.1 = (bf16[16,128,128]{2,1,0:T(8,128)(2,1)}, s32[32,1,256]{2,1,0:T(1,128)}, bf16[32,256,128]{2,1,0:T(8,128)(2,1)}) custom-call(bf16[16,128,128]{2,1,0:T(8,128)(2,1)} %pool.1.pooled_ref, s32[32,1,256]{2,1,0:T(1,128)} %broadcast_in_dim.23.ids_ref, s32[256,32]{1,0:T(8,128)} %copy.14.own_ids_ref, bf16[32,512,128]{2,1,0:T(8,128)(2,1)} %tables_ref.1), custom_call_target="tpu_custom_call" | custom-call | tf_op jit(solution)/shard_map/forward/pallas_call | solution.py:410
  44.6 26.9 %top.1 = (bf16[32,256,128]{2,1,0:T(8,128)(2,1)}, bf16[16,128,128]{2,1,0:T(8,128)(2,1)}) custom-call(s32[1]{0:T(128)} %bitcast.5.index_ref, s32[16,32]{1,0:T(8,128)} %sizes_ref.1, bf16[256,128]{1,0:T(8,128)(2,1)} %dense_ref.1, s32[256,1]{1,0:T(8,128)} %copy.15.labels_ref, bf16[32,256,128]{2,1,0:T(8,128)(2,1)} %get-tuple-element.8.small_ref, ...), custom_call_target="tpu_custom_call" | custom-call | tf_op jit(solution)/shard_map/top/pallas_call | solution.py:303
  71.5 0.0 copy-start.1
  71.5 3.8 %all-to-all-start = ((bf16[32,256,128]{2,1,0:T(8,128)(2,1)}), bf16[32,256,128]{2,1,0:T(8,128)(2,1)S(1)}, u32[]{:S(2)}, u32[]{:S(2)}) async-start(bf16[32,256,128]{2,1,0:T(8,128)(2,1)} %get-tuple-element.10), calls=%async_computation | async-start | bytes 4194304 | tf_op jit(solution)/shard_map/all_to_all | solution.py:635
  75.4 0.0 copy-done.1
  75.4 0.6 copy.18
  76.0 1.6 constant_dynamic-slice_fusion.table_ref
  77.5 65.4 %fold_exchange.1.fold_ref = bf16[32,128,128]{2,1,0:T(8,128)(2,1)} custom-call(bf16[16,128,128]{2,1,0:T(8,128)(2,1)} %get-tuple-element.11.fold_ref), custom_call_target="tpu_custom_call" | custom-call | flops 13421772800 | bytes 1048576 | tf_op jit(solution)/shard_map/fold_exchange/pallas_call | solution.py:488
  143.0 21.5 %scatter.1 = bf16[8192,128]{1,0:T(8,128)(2,1)} custom-call(s32[32,256]{1,0:T(8,128)} %bitcast.28, s32[32,128]{1,0:T(8,128)} %bitcast.25, s32[32,128]{1,0:T(8,128)} %bitcast.26, bf16[32,128,128]{2,1,0:T(8,128)(2,1)} %fold_exchange.1.fold_ref, bf16[8192,128]{1,0:T(8,128)(2,1)} %bitcast.19), custom_call_target="tpu_custom_call" | custom-call | flops 2684354560 | bytes 4194304 | tf_op jit(solution)/shard_map/scatter/pallas_call | solution.py:130
  164.4 0.0 all-to-all-done.grads_ref
  164.4 0.0 copy-start
  164.4 1.3 copy-done
  165.8 5.1 %small_update.1 = bf16[512,128]{1,0:T(8,128)(2,1)} custom-call(s32[1]{0:T(128)} %constant.7.clone.1.first_ref, s32[32,256]{1,0:T(8,128)} %bitcast.22, bf16[32,256,128]{2,1,0:T(8,128)(2,1)} %copy-done, bf16[512,128]{1,0:T(8,128)(2,1)} %constant_dynamic-slice_fusion.table_ref), custom_call_target="tpu_custom_call" | custom-call | tf_op jit(solution)/shard_map/small_update/pallas_call | solution.py:159
  170.9 34.9 %spread_all.1 = bf16[32,2,256,128]{3,2,1,0:T(8,128)(2,1)} custom-call(bf16[2,256,128]{2,1,0:T(8,128)(2,1)} %bitcast.20), custom_call_target="tpu_custom_call" | custom-call | tf_op jit(solution)/shard_map/spread_all/pallas_call | solution.py:593
  205.8 4.7 %copy.20 = bf16[32,512,128]{2,1,0:T(8,128)(2,1)} copy(bf16[32,512,128]{2,1,0:T(8,128)(2,1)} %bitcast.16) | data formatting | bytes 8388608
Async XLA Ops:
  71.5 3.8 %copy-start.1 = (s32[32,1,256]{2,1,0:T(1,128)S(1)}, s32[32,1,256]{2,1,0:T(1,128)}, u32[]{:S(2)}) copy-start(s32[32,1,256]{2,1,0:T(1,128)} %get-tuple-element.7) | copy-start | bytes 98308
  71.5 92.9 %all-to-all-start = ((bf16[32,256,128]{2,1,0:T(8,128)(2,1)}), bf16[32,256,128]{2,1,0:T(8,128)(2,1)S(1)}, u32[]{:S(2)}, u32[]{:S(2)}) async-start(bf16[32,256,128]{2,1,0:T(8,128)(2,1)} %get-tuple-element.10), calls=%async_computation | async-start | bytes 4194304 | tf_op jit(solution)/shard_map/all_to_all | solution.py:635
  164.4 1.3 copy-start

commit v4 on v3

--- a/solution.py
+++ b/solution.py
@@ -235,6 +235,9 @@
             pairs[start : start + chunk, at_tile * LANES : pair_pad] = (tile * scale).astype(bf16)
 
     block = 128
+    labels_col = jnp.transpose(
+        jnp.broadcast_to(labels_ref[...].astype(f32), (LANES, batch))
+    )[:, 0:1]
     for start in range(0, batch, block):
         at = slice(start, start + block)
         preact = (
@@ -244,7 +247,7 @@
         )
         squash = jax.nn.sigmoid(preact)
         logits = jnp.sum(preact * squash * wout_ref[...], axis=1, keepdims=True)
-        grad = jax.nn.sigmoid(logits) - labels_ref[at, :].astype(f32)
+        grad = jax.nn.sigmoid(logits) - labels_col[at, :]
         pre_grad = (
             grad * wout_ref[...] * (squash * (1.0 + preact * (1.0 - squash)))
         ).astype(bf16)
@@ -317,7 +320,7 @@
         compiler_params=pltpu.CompilerParams(vmem_limit_bytes=VMEM_LIMIT),
         name="top",
     )(
-        index, sizes, dense, labels[:, None], small, large, w_first,
+        index, sizes, dense, labels[None, :], small, large, w_first,
         bias[None, :], wout[None, :],
     )
 
@@ -349,7 +352,7 @@
 
 def forward_kernel(
     pooled_ref, ids_ref, own_ids_ref, tables_ref, large_out, ids_out, small_out,
-    send, recv, id_send, id_recv, own,
+    send, recv, id_send, id_recv, own, tables,
 ):
     copies, groups = lax.axis_size("rep"), lax.axis_size("shard")
     devices = copies * groups
@@ -385,6 +388,8 @@
 
         lax.fori_loop(low, high, body, 0)
 
+    fetch = pltpu.make_async_copy(tables_ref, tables, own.at[2])
+    fetch.start()
     greet_all()
     run(1, groups, lambda k: block(k).start())
     run(1, devices, lambda k: ids(k).start())
@@ -394,9 +399,10 @@
     mine_ids.start()
     batch, small_count = own_ids_ref.shape
     rows = iota((batch, tables_ref.shape[1]), 1)
+    fetch.wait()
     for t in range(small_count):
         hot = (own_ids_ref[:, t : t + 1] == rows).astype(f32).astype(bf16)
-        small_out[t] = jnp.dot(hot, tables_ref[t], preferred_element_type=f32).astype(bf16)
+        small_out[t] = jnp.dot(hot, tables[t], preferred_element_type=f32).astype(bf16)
     mine.wait()
     mine_ids.wait()
     run(1, groups, lambda k: block_in(k).wait_recv())
@@ -416,11 +422,11 @@
                 (tables.shape[0], own_ids.shape[0], tables.shape[2]), tables.dtype
             ),
         ),
-        in_specs=[whole(pltpu.VMEM)] * 4,
+        in_specs=[whole(pltpu.VMEM)] * 3 + [whole(pl.ANY)],
         out_specs=(whole(pltpu.VMEM),) * 3,
         scratch_shapes=[pltpu.SemaphoreType.DMA((groups,))] * 2
         + [pltpu.SemaphoreType.DMA((devices,))] * 2
-        + [pltpu.SemaphoreType.DMA((2,))],
+        + [pltpu.SemaphoreType.DMA((3,)), pltpu.VMEM(tables.shape, tables.dtype)],
         compiler_params=pltpu.CompilerParams(
             collective_id=0, has_side_effects=True, vmem_limit_bytes=VMEM_LIMIT
         ),
@@ -632,6 +638,7 @@
     )
     fold_all = fold_exchange(fold, copies)
     sent = jnp.repeat(small_grads, per_table, axis=0)
+    sent, fold_all = lax.optimization_barrier((sent, fold_all))
     arrived = lax.all_to_all(sent, ("rep", "shard"), split_axis=0, concat_axis=0, tiled=True)
     large_new = scatter(rows, ends, fold_all, table)
     part_rows = small_count * small_rows // devices

time: 211 us -> 190 us (0.900)
  Pallas kernels: 193 us -> 147 us
  waiting for transfers between devices: 0.01 us -> 25.3 us
  starting transfers between devices: 3.8 us -> 6.29 us
    pallas_call x1, Pallas kernels: 65.4 us -> 24 us  [fold_exchange(): pl.pallas_call(fold_kernel, out_shape=jax.ShapeDtypeStruct((copies * grou...]
    all_to_all x1, waiting for transfers between devices: 0.01 us -> 25.3 us  [shards(): lax.all_to_all(sent, ('rep', 'shard'), split_axis=0, concat_axis=0, tiled...]
    pallas_call x1, Pallas kernels: 34.9 us -> 30.4 us  [spread_all(): pl.pallas_call(spread_kernel, out_shape=jax.ShapeDtypeStruct((devices, 2,...]
    all_to_all x1, starting transfers between devices: 3.8 us -> 6.29 us  [shards(): lax.all_to_all(sent, ('rep', 'shard'), split_axis=0, concat_axis=0, tiled...]
  transfers between devices with their start and end apart: 1 -> 1, of which waited for: 0 -> 1; matrix products, arithmetic and copies ran while one was open for 1% -> 1% of each run, Pallas kernels for 41% -> 12%
where the time goes in v4:
time: 190 us; the launch traced here: 191 us
  Pallas kernels  147 us (77%)
  waiting for transfers between devices  25.3 us (13%)
  local copies, waits for them, and re-layouts  11 us (6%)
  starting transfers between devices  6.29 us (3%)
    pallas_call x1, Pallas kernels, spread_all(): pl.pallas_call(spread_kernel, out_shape=jax.ShapeDtypeStruct((devices, 2,...  30.4 us
    pallas_call x1, Pallas kernels, forward(): pl.pallas_call(forward_kernel, out_shape=(jax.ShapeDtypeStruct(pooled.sha...  26.9 us
    pallas_call x1, Pallas kernels, top(): pl.pallas_call(functools.partial(top_kernel, vec_count, pad), out_shape=(...  26.9 us
    all_to_all x1, waiting for transfers between devices, shards(): lax.all_to_all(sent, ('rep', 'shard'), split_axis=0, concat_axis=0, tiled...  25.3 us
    pallas_call x1, Pallas kernels, fold_exchange(): pl.pallas_call(fold_kernel, out_shape=jax.ShapeDtypeStruct((copies * grou...  24 us
    pallas_call x1, Pallas kernels, scatter(): pl.pallas_call(scatter_kernel, out_shape=jax.ShapeDtypeStruct(table.shape...  22.4 us
    pallas_call x1, Pallas kernels, pool(): pl.pallas_call(pool_kernel, out_shape=jax.ShapeDtypeStruct((owners, ends....  11.6 us
    unnamed x7, local copies, waits for them, and re-layouts  8.1 us
  transfers between devices with their start and end apart: 1, of which 1 were waited for; matrix products, arithmetic and copies ran while one was open for 1% of the time, Pallas kernels for 12%

profile of v4, /device:TPU:0, one launch (start us, length us, event | category | flops | bytes accessed | tf_op | source)
XLA Modules:
  0.0 190.7 jit_solution(16611614577409539512)
XLA Ops:
  0.6 1.5 copy.13.own_ids_ref
  2.1 1.4 broadcast_in_dim.23.ids_ref
  3.5 11.6 %pool.1.pooled_ref = bf16[16,128,128]{2,1,0:T(8,128)(2,1)} custom-call(s32[1]{0:T(128)} %bitcast.first_ref, s32[32,256]{1,0:T(8,128)} %bitcast.27, s32[32,128]{1,0:T(8,128)} %bitcast.23, s32[32,128]{1,0:T(8,128)} %bitcast.24, bf16[8192,128]{1,0:T(8,128)(2,1)} %bitcast.18), custom_call_target="tpu_custom_call" | custom-call | tf_op jit(solution)/shard_map/pool/pallas_call | solution.py:68
  15.2 26.9 %forward.1 = (bf16[16,128,128]{2,1,0:T(8,128)(2,1)}, s32[32,1,256]{2,1,0:T(1,128)}, bf16[32,256,128]{2,1,0:T(8,128)(2,1)}) custom-call(bf16[16,128,128]{2,1,0:T(8,128)(2,1)} %pool.1.pooled_ref, s32[32,1,256]{2,1,0:T(1,128)} %broadcast_in_dim.23.ids_ref, s32[256,32]{1,0:T(8,128)} %copy.13.own_ids_ref, bf16[32,512,128]{2,1,0:T(8,128)(2,1)} %tables_ref.1), custom_call_target="tpu_custom_call" | custom-call | tf_op jit(solution)/shard_map/forward/pallas_call | solution.py:416
  42.1 26.9 %top.1 = (bf16[32,256,128]{2,1,0:T(8,128)(2,1)}, bf16[16,128,128]{2,1,0:T(8,128)(2,1)}) custom-call(s32[1]{0:T(128)} %bitcast.5.index_ref, s32[16,32]{1,0:T(8,128)} %sizes_ref.1, bf16[256,128]{1,0:T(8,128)(2,1)} %dense_ref.1, s32[1,256]{1,0:T(1,128)} %bitcast.31, bf16[32,256,128]{2,1,0:T(8,128)(2,1)} %get-tuple-element.10.small_ref, ...), custom_call_target="tpu_custom_call" | custom-call | tf_op jit(solution)/shard_map/top/pallas_call | solution.py:306
  69.0 24.0 %fold_exchange.1.fold_ref = bf16[32,128,128]{2,1,0:T(8,128)(2,1)} custom-call(bf16[16,128,128]{2,1,0:T(8,128)(2,1)} %get-tuple-element.13.fold_ref), custom_call_target="tpu_custom_call" | custom-call | flops 13421772800 | bytes 1048576 | tf_op jit(solution)/shard_map/fold_exchange/pallas_call | solution.py:494
  93.0 0.0 copy-start.1
  93.0 6.3 %all-to-all-start = ((bf16[32,256,128]{2,1,0:T(8,128)(2,1)}), bf16[32,256,128]{2,1,0:T(8,128)(2,1)S(1)}, u32[]{:S(2)}, u32[]{:S(2)}) async-start(bf16[32,256,128]{2,1,0:T(8,128)(2,1)} %get-tuple-element.14), calls=%async_computation | async-start | bytes 4194304 | tf_op jit(solution)/shard_map/all_to_all | solution.py:642
  99.3 0.0 copy-done.1
  99.3 0.6 copy.16
  99.9 1.6 constant_dynamic-slice_fusion.table_ref
  101.5 22.4 %scatter.1 = bf16[8192,128]{1,0:T(8,128)(2,1)} custom-call(s32[32,256]{1,0:T(8,128)} %bitcast.28, s32[32,128]{1,0:T(8,128)} %bitcast.25, s32[32,128]{1,0:T(8,128)} %bitcast.26, bf16[32,128,128]{2,1,0:T(8,128)(2,1)} %fold_exchange.1.fold_ref, bf16[8192,128]{1,0:T(8,128)(2,1)} %bitcast.19), custom_call_target="tpu_custom_call" | custom-call | flops 2684354560 | bytes 4194304 | tf_op jit(solution)/shard_map/scatter/pallas_call | solution.py:130
  123.9 25.3 %all-to-all-done.grads_ref = bf16[32,256,128]{2,1,0:T(8,128)(2,1)S(1)} async-done(((bf16[32,256,128]{2,1,0:T(8,128)(2,1)}), bf16[32,256,128]{2,1,0:T(8,128)(2,1)S(1)}, u32[]{:S(2)}, u32[]{:S(2)}) %all-to-all-start) | async-done | bytes 2097184 | tf_op jit(solution)/shard_map/all_to_all | solution.py:642
  149.2 0.0 copy-start
  149.2 1.3 copy-done
  150.5 5.1 %small_update.1 = bf16[512,128]{1,0:T(8,128)(2,1)} custom-call(s32[1]{0:T(128)} %constant.7.clone.1.first_ref, s32[32,256]{1,0:T(8,128)} %bitcast.22, bf16[32,256,128]{2,1,0:T(8,128)(2,1)} %copy-done, bf16[512,128]{1,0:T(8,128)(2,1)} %constant_dynamic-slice_fusion.table_ref), custom_call_target="tpu_custom_call" | custom-call | tf_op jit(solution)/shard_map/small_update/pallas_call | solution.py:159
  155.7 30.4 %spread_all.1 = bf16[32,2,256,128]{3,2,1,0:T(8,128)(2,1)} custom-call(bf16[2,256,128]{2,1,0:T(8,128)(2,1)} %bitcast.20), custom_call_target="tpu_custom_call" | custom-call | tf_op jit(solution)/shard_map/spread_all/pallas_call | solution.py:599
  186.0 4.7 %copy.18 = bf16[32,512,128]{2,1,0:T(8,128)(2,1)} copy(bf16[32,512,128]{2,1,0:T(8,128)(2,1)} %bitcast.16) | data formatting | bytes 8388608
Async XLA Ops:
  93.0 6.3 %copy-start.1 = (s32[32,1,256]{2,1,0:T(1,128)S(1)}, s32[32,1,256]{2,1,0:T(1,128)}, u32[]{:S(2)}) copy-start(s32[32,1,256]{2,1,0:T(1,128)} %get-tuple-element.9) | copy-start | bytes 98308
  93.0 56.2 %all-to-all-start = ((bf16[32,256,128]{2,1,0:T(8,128)(2,1)}), bf16[32,256,128]{2,1,0:T(8,128)(2,1)S(1)}, u32[]{:S(2)}, u32[]{:S(2)}) async-start(bf16[32,256,128]{2,1,0:T(8,128)(2,1)} %get-tuple-element.14), calls=%async_computation | async-start | bytes 4194304 | tf_op jit(solution)/shard_map/all_to_all | solution.py:642
  149.2 1.3 copy-start

commit v5 on v4

--- a/solution.py
+++ b/solution.py
@@ -29,7 +29,15 @@
     return ((places >= starts) & (places < ends)).astype(f32).astype(bf16)
 
 
-def pool_kernel(first_ref, rows_ref, count_ref, ends_ref, table_ref, out_ref, wide, picked):
+def pool_kernel(
+    first_ref, rows_ref, count_ref, ends_ref, table_ref, ids_ref, out_ref, by_table, by_sample,
+    wide, picked,
+):
+    by_sample[...] = jnp.transpose(ids_ref[...])
+    per_table = by_table.shape[0] // ids_ref.shape[0]
+    for n in range(by_table.shape[0]):
+        t = n // per_table
+        by_table[n] = ids_ref[t : t + 1, :]
     slots = rows_ref.shape[1]
     owners = out_ref.shape[0]
     last = count_ref.shape[1] - 1
@@ -62,21 +70,25 @@
     lax.fori_loop(0, owners, sums, 0, unroll=4)
 
 
-def pool(first, owners, rows, ends, table):
+def pool(first, owners, rows, ends, table, ids, devices):
     slots = rows.shape[1]
     width = table.shape[1]
     return pl.pallas_call(
         pool_kernel,
-        out_shape=jax.ShapeDtypeStruct((owners, ends.shape[1], width), bf16),
-        in_specs=[whole(pltpu.SMEM)] * 3 + [whole(pltpu.VMEM)] * 2,
-        out_specs=whole(pltpu.VMEM),
+        out_shape=(
+            jax.ShapeDtypeStruct((owners, ends.shape[1], width), bf16),
+            jax.ShapeDtypeStruct((devices, 1, ids.shape[1]), ids.dtype),
+            jax.ShapeDtypeStruct((ids.shape[1], ids.shape[0]), ids.dtype),
+        ),
+        in_specs=[whole(pltpu.SMEM)] * 3 + [whole(pltpu.VMEM)] * 3,
+        out_specs=(whole(pltpu.VMEM),) * 3,
         scratch_shapes=[
             pltpu.VMEM(table.shape, f32),
             pltpu.VMEM((owners * slots, width), f32),
         ],
         compiler_params=pltpu.CompilerParams(vmem_limit_bytes=VMEM_LIMIT),
         name="pool",
-    )(first, rows, ends, ends, table)
+    )(first, rows, ends, ends, table, ids)
 
 
 def scatter_kernel(rows_ref, count_ref, ends_ref, fold_ref, table_ref, out_ref, spread, *sums):
@@ -630,9 +642,10 @@
     per_table = devices // small_count
     ends, rows, table = bag_ends[0], owner_row_index[0], large_tables[0]
 
-    sent_ids = jnp.repeat(jnp.transpose(small_ids), per_table, axis=0)[:, None]
-    pooled = pool(first[None], groups, rows, ends, table)
-    large, all_ids, small = forward(pooled, sent_ids, small_ids, small_tables)
+    pooled, sent_ids, own_ids = pool(
+        first[None], groups, rows, ends, table, jnp.transpose(small_ids), devices
+    )
+    large, all_ids, small = forward(pooled, sent_ids, own_ids, small_tables)
     small_grads, fold = top(
         index[None], batch_sizes, dense, labels, small, large, w_first, b_first, w_out
     )

time: 190 us -> 188 us (0.989)
  local copies, waits for them, and re-layouts: 11 us -> 8.14 us
    unnamed x7 -> x6, local copies, waits for them, and re-layouts: 8.1 us -> 6.58 us
where the time goes in v5:
time: 188 us
  Pallas kernels  148 us (79%)
  waiting for transfers between devices  25.1 us (13%)
  local copies, waits for them, and re-layouts  8.14 us (4%)
  starting transfers between devices  6.44 us (3%)
    pallas_call x1, Pallas kernels, spread_all(): pl.pallas_call(spread_kernel, out_shape=jax.ShapeDtypeStruct((devices, 2,...  30.4 us
    pallas_call x1, Pallas kernels, forward(): pl.pallas_call(forward_kernel, out_shape=(jax.ShapeDtypeStruct(pooled.sha...  28.1 us
    pallas_call x1, Pallas kernels, top(): pl.pallas_call(functools.partial(top_kernel, vec_count, pad), out_shape=(...  26.9 us
    all_to_all x1, waiting for transfers between devices, shards(): lax.all_to_all(sent, ('rep', 'shard'), split_axis=0, concat_axis=0, tiled...  25.1 us
    pallas_call x1, Pallas kernels, fold_exchange(): pl.pallas_call(fold_kernel, out_shape=jax.ShapeDtypeStruct((copies * grou...  24.1 us
    pallas_call x1, Pallas kernels, scatter(): pl.pallas_call(scatter_kernel, out_shape=jax.ShapeDtypeStruct(table.shape...  22.6 us
    pallas_call x1, Pallas kernels, pool(): pl.pallas_call(pool_kernel, out_shape=(jax.ShapeDtypeStruct((owners, ends...  10.4 us
    unnamed x6, local copies, waits for them, and re-layouts  6.58 us
  transfers between devices with their start and end apart: 1, of which 1 were waited for; matrix products, arithmetic and copies ran while one was open for 1% of the time, Pallas kernels for 12%

profile of v5, /device:TPU:0, one launch (start us, length us, event | category | flops | bytes accessed | tf_op | source)
XLA Modules:
  0.0 187.9 jit_solution(6390055693599351718)
XLA Ops:
  0.6 10.4 %pool.1 = (bf16[16,128,128]{2,1,0:T(8,128)(2,1)}, s32[32,1,256]{2,1,0:T(1,128)}, s32[256,32]{1,0:T(8,128)}) custom-call(s32[1]{0:T(128)} %bitcast.first_ref, s32[32,256]{1,0:T(8,128)} %bitcast.27, s32[32,128]{1,0:T(8,128)} %bitcast.22, s32[32,128]{1,0:T(8,128)} %bitcast.23, bf16[8192,128]{1,0:T(8,128)(2,1)} %bitcast.18, s32[32,256]{1,0:T(8,128)} %bitcast.26), custom_call_target="tpu_custom_call" | custom-call | tf_op jit(solution)/shard_map/pool/pallas_call | solution.py:76
  11.0 28.1 %forward.1 = (bf16[16,128,128]{2,1,0:T(8,128)(2,1)}, s32[32,1,256]{2,1,0:T(1,128)}, bf16[32,256,128]{2,1,0:T(8,128)(2,1)}) custom-call(bf16[16,128,128]{2,1,0:T(8,128)(2,1)} %get-tuple-element.12.pooled_ref, s32[32,1,256]{2,1,0:T(1,128)} %get-tuple-element.13.ids_ref, s32[256,32]{1,0:T(8,128)} %get-tuple-element.14.own_ids_ref, bf16[32,512,128]{2,1,0:T(8,128)(2,1)} %tables_ref.1), custom_call_target="tpu_custom_call" | custom-call | tf_op jit(solution)/shard_map/forward/pallas_call | solution.py:428
  39.2 26.9 %top.1 = (bf16[32,256,128]{2,1,0:T(8,128)(2,1)}, bf16[16,128,128]{2,1,0:T(8,128)(2,1)}) custom-call(s32[1]{0:T(128)} %bitcast.5.index_ref, s32[16,32]{1,0:T(8,128)} %sizes_ref.1, bf16[256,128]{1,0:T(8,128)(2,1)} %dense_ref.1, s32[1,256]{1,0:T(1,128)} %bitcast.31, bf16[32,256,128]{2,1,0:T(8,128)(2,1)} %get-tuple-element.16.small_ref, ...), custom_call_target="tpu_custom_call" | custom-call | tf_op jit(solution)/shard_map/top/pallas_call | solution.py:318
  66.0 24.1 %fold_exchange.1.fold_ref = bf16[32,128,128]{2,1,0:T(8,128)(2,1)} custom-call(bf16[16,128,128]{2,1,0:T(8,128)(2,1)} %get-tuple-element.19.fold_ref), custom_call_target="tpu_custom_call" | custom-call | flops 13421772800 | bytes 1048576 | tf_op jit(solution)/shard_map/fold_exchange/pallas_call | solution.py:506
  90.1 0.0 copy-start.1
  90.1 6.4 %all-to-all-start = ((bf16[32,256,128]{2,1,0:T(8,128)(2,1)}), bf16[32,256,128]{2,1,0:T(8,128)(2,1)S(1)}, u32[]{:S(2)}, u32[]{:S(2)}) async-start(bf16[32,256,128]{2,1,0:T(8,128)(2,1)} %get-tuple-element.20), calls=%async_computation | async-start | bytes 4194304 | tf_op jit(solution)/shard_map/all_to_all | solution.py:655
  96.6 0.0 copy-done.1
  96.6 0.6 copy.15
  97.2 1.6 constant_dynamic-slice_fusion.table_ref
  98.7 22.6 %scatter.1 = bf16[8192,128]{1,0:T(8,128)(2,1)} custom-call(s32[32,256]{1,0:T(8,128)} %bitcast.28, s32[32,128]{1,0:T(8,128)} %bitcast.24, s32[32,128]{1,0:T(8,128)} %bitcast.25, bf16[32,128,128]{2,1,0:T(8,128)(2,1)} %fold_exchange.1.fold_ref, bf16[8192,128]{1,0:T(8,128)(2,1)} %bitcast.19), custom_call_target="tpu_custom_call" | custom-call | flops 2684354560 | bytes 4194304 | tf_op jit(solution)/shard_map/scatter/pallas_call | solution.py:142
  121.3 25.1 %all-to-all-done.grads_ref = bf16[32,256,128]{2,1,0:T(8,128)(2,1)S(1)} async-done(((bf16[32,256,128]{2,1,0:T(8,128)(2,1)}), bf16[32,256,128]{2,1,0:T(8,128)(2,1)S(1)}, u32[]{:S(2)}, u32[]{:S(2)}) %all-to-all-start) | async-done | bytes 2097184 | tf_op jit(solution)/shard_map/all_to_all | solution.py:655
  146.4 0.0 copy-start
  146.4 1.3 copy-done
  147.8 5.2 %small_update.1 = bf16[512,128]{1,0:T(8,128)(2,1)} custom-call(s32[1]{0:T(128)} %constant.7.clone.1.first_ref, s32[32,256]{1,0:T(8,128)} %bitcast.21, bf16[32,256,128]{2,1,0:T(8,128)(2,1)} %copy-done, bf16[512,128]{1,0:T(8,128)(2,1)} %constant_dynamic-slice_fusion.table_ref), custom_call_target="tpu_custom_call" | custom-call | tf_op jit(solution)/shard_map/small_update/pallas_call | solution.py:171
  152.9 30.4 %spread_all.1 = bf16[32,2,256,128]{3,2,1,0:T(8,128)(2,1)} custom-call(bf16[2,256,128]{2,1,0:T(8,128)(2,1)} %bitcast.20), custom_call_target="tpu_custom_call" | custom-call | tf_op jit(solution)/shard_map/spread_all/pallas_call | solution.py:611
  183.3 4.7 %copy.17 = bf16[32,512,128]{2,1,0:T(8,128)(2,1)} copy(bf16[32,512,128]{2,1,0:T(8,128)(2,1)} %bitcast.16) | data formatting | bytes 8388608
Async XLA Ops:
  90.1 6.5 %copy-start.1 = (s32[32,1,256]{2,1,0:T(1,128)S(1)}, s32[32,1,256]{2,1,0:T(1,128)}, u32[]{:S(2)}) copy-start(s32[32,1,256]{2,1,0:T(1,128)} %get-tuple-element.15) | copy-start | bytes 98308
  90.1 56.3 %all-to-all-start = ((bf16[32,256,128]{2,1,0:T(8,128)(2,1)}), bf16[32,256,128]{2,1,0:T(8,128)(2,1)S(1)}, u32[]{:S(2)}, u32[]{:S(2)}) async-start(bf16[32,256,128]{2,1,0:T(8,128)(2,1)} %get-tuple-element.20), calls=%async_computation | async-start | bytes 4194304 | tf_op jit(solution)/shard_map/all_to_all | solution.py:655
  146.4 1.3 copy-start
